TPU v7x, 128 devices: a whole 4x4x4 slice. The times are simulated.
128 devices in a mesh: gx: 4 (over x), gy: 4 (over y), gz: 8 (over z, core).
Axes of the slice: x: 4, y: 4, z: 4, core: 2. Of those that a mesh axis runs over, the one named last changes fastest.
Arguments:
- positions: float32 [4096, 3, 256], P(('gx', 'gy', 'gz')), may hold values from 0 to 32, as said below
- smoothing: float32 [4096, 256], P(('gx', 'gy', 'gz')), may hold values from 0.35 to 2
- velocity: float32 [4096, 3, 256], P(('gx', 'gy', 'gz')), may hold values from -0.3 to 0.3
- counts: int32 [4096], P(('gx', 'gy', 'gz')), may hold values from 32 to 256
- plan_before: int32 [4096], P(('gx', 'gy', 'gz')), may hold values from 0 to 4095, as said below
- neighbours: int32 [4096, 8], P(('gx', 'gy', 'gz')), may hold values from 0 to 4095, as said below
- plan_after: int32 [4096], P(('gx', 'gy', 'gz')), may hold values from 0 to 4095, as said below
Outputs:
- new_positions: float32 [4096, 3, 256], P(('gx', 'gy', 'gz'))
- new_velocity: float32 [4096, 3, 256], P(('gx', 'gy', 'gz'))
- density: float32 [4096, 256], P(('gx', 'gy', 'gz'))
Inputs may be any that keep to these rules, and one draw needn't show every extreme that they name: `plan_before`: a permutation: each value once. The cells that device d holds (c // 32 = d) go to exactly 16 different devices (place // 32), exactly 2 cells to each. `plan_after`: a permutation of the places after plan_before, with the same property: the cells of one device go to exactly 16 devices, 2 to each. Every entry of row a lies on the device a // 32 or on one of its six face neighbours in the grid of devices (index = (gx * size of gy + gy) * size of gz + gz), which closes into a loop along each axis; entries may repeat and may name a itself. `positions`: coordinates inside the periodic box of the steps.
All inputs are finite; a program needn't handle non-finite values.
Results may differ from a plain program's by a relative error of at most 0.0003.
Values sent between devices are 32-bit elements; how exact they have to be, the bound alone decides.
A program may use at most 64 MiB of HBM per device.

v0:
```python
import jax
import jax.numpy as jnp
from jax import lax
from jax.sharding import PartitionSpec as P

time_step = 0.1


def split_up(array, dim, peers):
    before, after = (array.shape[:dim], array.shape[dim + 1 :])
    return jnp.moveaxis(array.reshape(*before, peers, -1, *after), dim, 0)


def joined_along(parts, dim):
    shape = list(parts.shape[1:])
    shape[dim] *= parts.shape[0]
    return jnp.moveaxis(parts, 0, dim).reshape(shape)


def one_exchange(array, axis, axes, splits, concats):
    sizes = [lax.axis_size(a) for a in axes]
    parts = split_up(array, splits[0], sizes[0])
    parts = jnp.moveaxis(split_up(parts, splits[1] + 1, sizes[1]), 0, 1)
    inside = parts.shape[2:]
    parts = parts.reshape(-1, *inside)
    parts = lax.all_to_all(parts, axis, split_axis=0, concat_axis=0, tiled=True)
    parts = joined_along(parts.reshape(*sizes, *inside), concats[0] + 1)
    return joined_along(parts, concats[1])


def with_halo(array, sides, width):
    edges = {}
    for axis, dim in sides:
        peers, length = (lax.axis_size(axis), array.shape[dim])
        up = [(i, (i + 1) % peers) for i in range(peers)]
        last = lax.slice_in_dim(array, length - width, length, axis=dim)
        leading = lax.slice_in_dim(array, 0, width, axis=dim)
        edges[dim] = (
            lax.ppermute(last, axis, up),
            lax.ppermute(leading, axis, [(b, a) for a, b in up]),
        )
    done = []
    for _, dim in sides:
        low, high = edges[dim]
        around = [(width, width) if d in done else (0, 0) for d in range(array.ndim)]
        array = jnp.concatenate([jnp.pad(low, around), array, jnp.pad(high, around)], axis=dim)
        done.append(dim)
    return array


def pair_offsets(own_pos, near_pos, box):
    offsets = []
    for component in range(3):
        length = box[component]
        raw = own_pos[:, component, :, None, None] - near_pos[:, None, :, component, :]
        offsets.append(jnp.mod(raw + 0.5 * length, length) - 0.5 * length)
    return offsets


def live_mask(near_count, particles):
    ladder = jnp.arange(particles).astype(jnp.float32)
    return (ladder[None, None, :] < near_count[:, :, None]).astype(jnp.float32)


def density_group(own_pos, own_h, near_pos, near_count, box):
    particles = own_pos.shape[-1]
    part_mass = 1.0 / (near_pos.shape[1] * particles)
    offsets = pair_offsets(own_pos, near_pos, box)
    dist_sq = offsets[0] * offsets[0] + offsets[1] * offsets[1] + offsets[2] * offsets[2]
    inv_area = 1.0 / (own_h * own_h)
    kernel = jnp.exp(-dist_sq * inv_area[:, :, None, None])
    weights = live_mask(near_count, particles)[:, None, :, :]
    total = jnp.sum(kernel * weights, axis=(2, 3))
    return part_mass * (1.0 + total) / (own_h * own_h * own_h)


def accel_group(own_pos, own_h, own_rho, near_pos, near_count, near_rho, box):
    particles = own_pos.shape[-1]
    part_mass = 1.0 / (near_pos.shape[1] * particles)
    offsets = pair_offsets(own_pos, near_pos, box)
    dist_sq = offsets[0] * offsets[0] + offsets[1] * offsets[1] + offsets[2] * offsets[2]
    inv_area = 1.0 / (own_h * own_h)
    kernel = jnp.exp(-dist_sq * inv_area[:, :, None, None])
    weights = live_mask(near_count, particles)
    pair_weight = (
        kernel * (weights / near_rho)[:, None, :, :]
        + kernel * weights[:, None, :, :] * (1.0 / own_rho)[:, :, None, None]
    )
    scale_term = 2.0 * part_mass / (own_h * own_h * own_h * own_h * own_h)
    parts = [
        jnp.sum(pair_weight * offsets[component], axis=(2, 3)) * scale_term
        for component in range(3)
    ]
    return jnp.stack(parts, axis=1)


def relocate(fields, plan):
    cell_count = plan.shape[0]
    devices = lax.axis_size("gx") * lax.axis_size("gy") * lax.axis_size("gz")
    capacity = max(2, cell_count // devices)
    target = plan // cell_count
    ladder = jnp.arange(cell_count, dtype=jnp.int32)
    earlier = (target[:, None] == target[None, :]) & (ladder[None, :] < ladder[:, None])
    slot_rank = jnp.sum(earlier.astype(jnp.int32), axis=1)
    send_slot = target * capacity + slot_rank
    buffer_rows = devices * capacity
    arrival = (plan % cell_count).astype(jnp.float32)
    marker = jnp.full((buffer_rows,), -1.0, jnp.float32).at[send_slot].set(arrival)
    packed = tuple(
        (
            jnp.zeros((buffer_rows,) + field.shape[1:], jnp.float32).at[send_slot].set(field)
            for field in fields
        )
    ) + (marker,)
    count_x = lax.axis_size("gx")
    sectioned = tuple(
        (item.reshape((count_x, devices // count_x, capacity) + item.shape[1:]) for item in packed)
    )
    received = jax.tree.map(
        lambda part: one_exchange(part, ("gx", "gy", "gz"), ("gx", ("gy", "gz")), (0, 1), (0, 1)),
        sectioned,
    )
    flat = tuple(
        (item.reshape((buffer_rows,) + source.shape[1:]) for item, source in zip(received, packed))
    )
    landing = flat[-1]
    place_index = jnp.where(landing >= 0.0, landing, float(cell_count)).astype(jnp.int32)
    placed = []
    for item in flat[:-1]:
        holder = jnp.zeros((cell_count,) + item.shape[1:], jnp.float32)
        placed.append(holder.at[place_index].set(item, mode="drop"))
    return tuple(placed)


def lookup(neighbours, cell_count):
    count_x, count_y, count_z = (lax.axis_size("gx"), lax.axis_size("gy"), lax.axis_size("gz"))
    index_x, index_y, index_z = (lax.axis_index("gx"), lax.axis_index("gy"), lax.axis_index("gz"))
    owner = neighbours // cell_count
    table_block = jnp.full(owner.shape, 13, jnp.int32)
    for step_x, step_y, step_z, location in (
        (-1, 0, 0, 4),
        (1, 0, 0, 22),
        (0, -1, 0, 10),
        (0, 1, 0, 16),
        (0, 0, -1, 12),
        (0, 0, 1, 14),
    ):
        device_id = (
            (index_x + step_x) % count_x * count_y + (index_y + step_y) % count_y
        ) * count_z + (index_z + step_z) % count_z
        table_block = jnp.where(owner == device_id, location, table_block)
    return table_block * cell_count + neighbours % cell_count


def shards(positions, smoothing, velocity, counts, plan_before, neighbours, plan_after):
    cell_count = positions.shape[0]
    particles = positions.shape[-1]
    box = (
        float(cell_count // 4 * lax.axis_size("gx")),
        float(2 * lax.axis_size("gy")),
        float(2 * lax.axis_size("gz")),
    )
    placed_pos, placed_h, placed_vel, placed_count = relocate(
        (positions, smoothing, velocity, counts.astype(jnp.float32)), plan_before
    )
    cycle_pos, cycle_count = (
        with_halo(
            placed_pos.reshape((1, 1, 1) + placed_pos.shape), (("gx", 0), ("gy", 1), ("gz", 2)), 1
        ),
        with_halo(placed_count.reshape(1, 1, 1, cell_count), (("gx", 0), ("gy", 1), ("gz", 2)), 1),
    )
    table_pos = cycle_pos.reshape(27 * cell_count, 3, particles)
    table_count = cycle_count.reshape(27 * cell_count)
    near_index = lookup(neighbours, cell_count)
    groups = cell_count // 4
    group_pos = placed_pos.reshape(groups, 4, 3, particles)
    group_h = placed_h.reshape(groups, 4, particles)
    group_count = placed_count.reshape(groups, 4)
    group_near = near_index.reshape(groups, 4, -1)

    def density_step(inputs):
        own_pos, own_h, own_count, near_ids = inputs
        near_pos = jnp.concatenate([own_pos[:, None], table_pos[near_ids]], axis=1)
        near_count = jnp.concatenate([own_count[:, None], table_count[near_ids]], axis=1)
        return density_group(own_pos, own_h, near_pos, near_count, box)

    rho = lax.map(density_step, (group_pos, group_h, group_count, group_near)).reshape(
        cell_count, particles
    )
    cycle_rho = with_halo(
        rho.reshape(1, 1, 1, cell_count, particles), (("gx", 0), ("gy", 1), ("gz", 2)), 1
    )
    table_rho = cycle_rho.reshape(27 * cell_count, particles)
    group_rho = rho.reshape(groups, 4, particles)

    def accel_step(inputs):
        own_pos, own_h, own_count, near_ids, own_rho = inputs
        near_pos = jnp.concatenate([own_pos[:, None], table_pos[near_ids]], axis=1)
        near_count = jnp.concatenate([own_count[:, None], table_count[near_ids]], axis=1)
        near_rho = jnp.concatenate([own_rho[:, None], table_rho[near_ids]], axis=1)
        return accel_group(own_pos, own_h, own_rho, near_pos, near_count, near_rho, box)

    accel = lax.map(accel_step, (group_pos, group_h, group_count, group_near, group_rho)).reshape(
        cell_count, 3, particles
    )
    kicked = placed_vel + time_step * accel
    drifted = placed_pos + time_step * kicked
    final_pos, final_vel, final_rho = relocate((drifted, kicked, rho), plan_after)
    return (final_pos, final_vel, final_rho)


def solution(mesh):
    in_specs = (
        P(("gx", "gy", "gz"), None, None),
        P(("gx", "gy", "gz"), None),
        P(("gx", "gy", "gz"), None, None),
        P(("gx", "gy", "gz")),
        P(("gx", "gy", "gz")),
        P(("gx", "gy", "gz"), None),
        P(("gx", "gy", "gz")),
    )
    out_specs = (
        P(("gx", "gy", "gz"), None, None),
        P(("gx", "gy", "gz"), None, None),
        P(("gx", "gy", "gz"), None),
    )
    return jax.shard_map(shards, mesh=mesh, in_specs=in_specs, out_specs=out_specs, check_vma=False)
```

profile of v0, /device:TPU:1, one launch (start us, length us, event | category | flops | bytes accessed | tf_op | source)
XLA Modules:
  0.0 630.5 jit_solution(7791354860644168810)
XLA Ops:
  3.0 11.5 %all-to-all-start.1 = ((f32[128,1,1,2]{3,2,1,0:T(1,128)}), f32[128,1,1,2]{3,2,1,0:T(1,128)S(1)}, u32[]{:S(2)}, u32[]{:S(2)}) async-start(f32[128,1,1,2]{3,2,1,0:T(1,128)} %bitcast.38), calls=%async_computation.1 | async-start | bytes 131072 | tf_op jit(solution)/shard_map/all_to_all | solution.py:26
  32.2 12.8 %all-to-all-done.2 = f32[128,1,1,2,3,256]{5,3,4,2,1,0:T(2,128)S(1)} async-done(((f32[128,1,1,2,3,256]{5,3,4,2,1,0:T(2,128)}), f32[128,1,1,2,3,256]{5,3,4,2,1,0:T(2,128)S(1)}, u32[]{:S(2)}, u32[]{:S(2)}) %all-to-all-start.2) | async-done | bytes 786464 | tf_op jit(solution)/shard_map/all_to_all | solution.py:26
  59.3 9.2 %all-to-all-start.4 = ((f32[128,1,1,2,256]{4,3,2,1,0:T(2,128)}), f32[128,1,1,2,256]{4,3,2,1,0:T(2,128)S(1)}, u32[]{:S(2)}, u32[]{:S(2)}) async-start(f32[128,1,1,2,256]{4,3,2,1,0:T(2,128)} %bitcast.60), calls=%async_computation.4 | async-start | bytes 524288 | tf_op jit(solution)/shard_map/all_to_all | solution.py:26
  99.3 200.9 %while.24 = (s32[]{:T(128)}, f32[8,4,256]{2,1,0:T(4,128)S(1)}, f32[8,4,3,256]{3,1,2,0:T(4,128)S(1)}, s32[8,4,8]{2,1,0:T(4,128)S(1)}, f32[864,3,256]{2,1,0:T(4,12...) while((s32[]{:T(128)}, f32[8,4,256]{2,1,0:T(4,128)S(1)}, ...), condition=%wide.region_14.15_spmd, body=%wide.region_12.14_spmd.sunk | while | flops 84988296 | bytes 1130465 | solution.py:187
  103.3 21.1 %fusion.101 = f32[4,256]{1,0:T(4,128)S(1)} fusion(f32[4,9,256]{2,1,0:T(8,128)S(1)} %compare_convert_fusion.4, f32[4,256]{1,0:T(4,128)S(1)} %fusion.99, f32[4,9,256]{2,1,0:T(8,128)S(1)} %copy.122, f32[4,256]{1,0:T(4,128)S(1)} %get-tuple-element.509, f32[4,9,256]{2,1,0:T(8,128)S(1)} %copy.123, f32[4,256]{1,0:T(4,128)S(1)} %get-tuple-element.511, ...), kind=kLoop, calls=%fused_computation.45.clone.1 | loop fusion | flops 84933632 | bytes 167936 | tf_op jit(solution)/shard_map/while/body/eval_jaxpr/reduce_sum | solution.py:73
  128.4 21.1 %fusion.101 = f32[4,256]{1,0:T(4,128)S(1)} fusion(f32[4,9,256]{2,1,0:T(8,128)S(1)} %compare_convert_fusion.4, f32[4,256]{1,0:T(4,128)S(1)} %fusion.99, f32[4,9,256]{2,1,0:T(8,128)S(1)} %copy.122, f32[4,256]{1,0:T(4,128)S(1)} %get-tuple-element.509, f32[4,9,256]{2,1,0:T(8,128)S(1)} %copy.123, f32[4,256]{1,0:T(4,128)S(1)} %get-tuple-element.511, ...), kind=kLoop, calls=%fused_computation.45.clone.1 | loop fusion | flops 84933632 | bytes 167936 | tf_op jit(solution)/shard_map/while/body/eval_jaxpr/reduce_sum | solution.py:73
  153.5 21.1 %fusion.101 = f32[4,256]{1,0:T(4,128)S(1)} fusion(f32[4,9,256]{2,1,0:T(8,128)S(1)} %compare_convert_fusion.4, f32[4,256]{1,0:T(4,128)S(1)} %fusion.99, f32[4,9,256]{2,1,0:T(8,128)S(1)} %copy.122, f32[4,256]{1,0:T(4,128)S(1)} %get-tuple-element.509, f32[4,9,256]{2,1,0:T(8,128)S(1)} %copy.123, f32[4,256]{1,0:T(4,128)S(1)} %get-tuple-element.511, ...), kind=kLoop, calls=%fused_computation.45.clone.1 | loop fusion | flops 84933632 | bytes 167936 | tf_op jit(solution)/shard_map/while/body/eval_jaxpr/reduce_sum | solution.py:73
  178.7 21.1 %fusion.101 = f32[4,256]{1,0:T(4,128)S(1)} fusion(f32[4,9,256]{2,1,0:T(8,128)S(1)} %compare_convert_fusion.4, f32[4,256]{1,0:T(4,128)S(1)} %fusion.99, f32[4,9,256]{2,1,0:T(8,128)S(1)} %copy.122, f32[4,256]{1,0:T(4,128)S(1)} %get-tuple-element.509, f32[4,9,256]{2,1,0:T(8,128)S(1)} %copy.123, f32[4,256]{1,0:T(4,128)S(1)} %get-tuple-element.511, ...), kind=kLoop, calls=%fused_computation.45.clone.1 | loop fusion | flops 84933632 | bytes 167936 | tf_op jit(solution)/shard_map/while/body/eval_jaxpr/reduce_sum | solution.py:73
  203.8 21.1 %fusion.101 = f32[4,256]{1,0:T(4,128)S(1)} fusion(f32[4,9,256]{2,1,0:T(8,128)S(1)} %compare_convert_fusion.4, f32[4,256]{1,0:T(4,128)S(1)} %fusion.99, f32[4,9,256]{2,1,0:T(8,128)S(1)} %copy.122, f32[4,256]{1,0:T(4,128)S(1)} %get-tuple-element.509, f32[4,9,256]{2,1,0:T(8,128)S(1)} %copy.123, f32[4,256]{1,0:T(4,128)S(1)} %get-tuple-element.511, ...), kind=kLoop, calls=%fused_computation.45.clone.1 | loop fusion | flops 84933632 | bytes 167936 | tf_op jit(solution)/shard_map/while/body/eval_jaxpr/reduce_sum | solution.py:73
  228.9 21.1 %fusion.101 = f32[4,256]{1,0:T(4,128)S(1)} fusion(f32[4,9,256]{2,1,0:T(8,128)S(1)} %compare_convert_fusion.4, f32[4,256]{1,0:T(4,128)S(1)} %fusion.99, f32[4,9,256]{2,1,0:T(8,128)S(1)} %copy.122, f32[4,256]{1,0:T(4,128)S(1)} %get-tuple-element.509, f32[4,9,256]{2,1,0:T(8,128)S(1)} %copy.123, f32[4,256]{1,0:T(4,128)S(1)} %get-tuple-element.511, ...), kind=kLoop, calls=%fused_computation.45.clone.1 | loop fusion | flops 84933632 | bytes 167936 | tf_op jit(solution)/shard_map/while/body/eval_jaxpr/reduce_sum | solution.py:73
  254.0 21.1 %fusion.101 = f32[4,256]{1,0:T(4,128)S(1)} fusion(f32[4,9,256]{2,1,0:T(8,128)S(1)} %compare_convert_fusion.4, f32[4,256]{1,0:T(4,128)S(1)} %fusion.99, f32[4,9,256]{2,1,0:T(8,128)S(1)} %copy.122, f32[4,256]{1,0:T(4,128)S(1)} %get-tuple-element.509, f32[4,9,256]{2,1,0:T(8,128)S(1)} %copy.123, f32[4,256]{1,0:T(4,128)S(1)} %get-tuple-element.511, ...), kind=kLoop, calls=%fused_computation.45.clone.1 | loop fusion | flops 84933632 | bytes 167936 | tf_op jit(solution)/shard_map/while/body/eval_jaxpr/reduce_sum | solution.py:73
  279.1 21.1 %fusion.101 = f32[4,256]{1,0:T(4,128)S(1)} fusion(f32[4,9,256]{2,1,0:T(8,128)S(1)} %compare_convert_fusion.4, f32[4,256]{1,0:T(4,128)S(1)} %fusion.99, f32[4,9,256]{2,1,0:T(8,128)S(1)} %copy.122, f32[4,256]{1,0:T(4,128)S(1)} %get-tuple-element.509, f32[4,9,256]{2,1,0:T(8,128)S(1)} %copy.123, f32[4,256]{1,0:T(4,128)S(1)} %get-tuple-element.511, ...), kind=kLoop, calls=%fused_computation.45.clone.1 | loop fusion | flops 84933632 | bytes 167936 | tf_op jit(solution)/shard_map/while/body/eval_jaxpr/reduce_sum | solution.py:73
  326.2 232.9 %while.25 = (s32[]{:T(128)}, f32[8,4,3,256]{3,1,2,0:T(4,128)S(1)}, f32[8,4,3,256]{3,1,2,0:T(4,128)S(1)}, s32[8,4,8]{2,1,0:T(4,128)S(1)}, f32[864,3,256]{2,1,0:T(...) while((s32[]{:T(128)}, f32[8,4,3,256]{3,1,2,0:T(4,128)S(1)}, ...), condition=%wide.region_19.20_spmd, body=%wide.region_15.19_spmd.sunk | while | flops 103907720 | bytes 1381641 | solution.py:203
  330.9 24.3 %multiply_reduce_fusion.4 = (f32[4,256]{1,0:T(4,128)S(1)}, f32[4,256]{1,0:T(4,128)S(1)}, f32[4,256]{1,0:T(4,128)S(1)}) fusion(f32[4,9,256]{2,1,0:T(8,128)S(1)} %copy.126, f32[4,256]{1,0:T(4,128)S(1)} %get-tuple-element.527, f32[4,256]{1,0:T(4,128)S(1)} %get-tuple-element.528, f32[4,9,256]{2,1,0:T(8,128)S(1)} %compare_convert_fusion.5, ...), kind=kLoop, calls=%fused_computation.84.clone.1 | loop fusion | flops 103805952 | bytes 217088 | tf_op jit(solution)/shard_map/while/body/eval_jaxpr/reduce_sum | solution.py:91
  360.0 24.3 %multiply_reduce_fusion.4 = (f32[4,256]{1,0:T(4,128)S(1)}, f32[4,256]{1,0:T(4,128)S(1)}, f32[4,256]{1,0:T(4,128)S(1)}) fusion(f32[4,9,256]{2,1,0:T(8,128)S(1)} %copy.126, f32[4,256]{1,0:T(4,128)S(1)} %get-tuple-element.527, f32[4,256]{1,0:T(4,128)S(1)} %get-tuple-element.528, f32[4,9,256]{2,1,0:T(8,128)S(1)} %compare_convert_fusion.5, ...), kind=kLoop, calls=%fused_computation.84.clone.1 | loop fusion | flops 103805952 | bytes 217088 | tf_op jit(solution)/shard_map/while/body/eval_jaxpr/reduce_sum | solution.py:91
  389.1 24.3 %multiply_reduce_fusion.4 = (f32[4,256]{1,0:T(4,128)S(1)}, f32[4,256]{1,0:T(4,128)S(1)}, f32[4,256]{1,0:T(4,128)S(1)}) fusion(f32[4,9,256]{2,1,0:T(8,128)S(1)} %copy.126, f32[4,256]{1,0:T(4,128)S(1)} %get-tuple-element.527, f32[4,256]{1,0:T(4,128)S(1)} %get-tuple-element.528, f32[4,9,256]{2,1,0:T(8,128)S(1)} %compare_convert_fusion.5, ...), kind=kLoop, calls=%fused_computation.84.clone.1 | loop fusion | flops 103805952 | bytes 217088 | tf_op jit(solution)/shard_map/while/body/eval_jaxpr/reduce_sum | solution.py:91
  418.2 24.3 %multiply_reduce_fusion.4 = (f32[4,256]{1,0:T(4,128)S(1)}, f32[4,256]{1,0:T(4,128)S(1)}, f32[4,256]{1,0:T(4,128)S(1)}) fusion(f32[4,9,256]{2,1,0:T(8,128)S(1)} %copy.126, f32[4,256]{1,0:T(4,128)S(1)} %get-tuple-element.527, f32[4,256]{1,0:T(4,128)S(1)} %get-tuple-element.528, f32[4,9,256]{2,1,0:T(8,128)S(1)} %compare_convert_fusion.5, ...), kind=kLoop, calls=%fused_computation.84.clone.1 | loop fusion | flops 103805952 | bytes 217088 | tf_op jit(solution)/shard_map/while/body/eval_jaxpr/reduce_sum | solution.py:91
  447.4 24.3 %multiply_reduce_fusion.4 = (f32[4,256]{1,0:T(4,128)S(1)}, f32[4,256]{1,0:T(4,128)S(1)}, f32[4,256]{1,0:T(4,128)S(1)}) fusion(f32[4,9,256]{2,1,0:T(8,128)S(1)} %copy.126, f32[4,256]{1,0:T(4,128)S(1)} %get-tuple-element.527, f32[4,256]{1,0:T(4,128)S(1)} %get-tuple-element.528, f32[4,9,256]{2,1,0:T(8,128)S(1)} %compare_convert_fusion.5, ...), kind=kLoop, calls=%fused_computation.84.clone.1 | loop fusion | flops 103805952 | bytes 217088 | tf_op jit(solution)/shard_map/while/body/eval_jaxpr/reduce_sum | solution.py:91
  476.5 24.3 %multiply_reduce_fusion.4 = (f32[4,256]{1,0:T(4,128)S(1)}, f32[4,256]{1,0:T(4,128)S(1)}, f32[4,256]{1,0:T(4,128)S(1)}) fusion(f32[4,9,256]{2,1,0:T(8,128)S(1)} %copy.126, f32[4,256]{1,0:T(4,128)S(1)} %get-tuple-element.527, f32[4,256]{1,0:T(4,128)S(1)} %get-tuple-element.528, f32[4,9,256]{2,1,0:T(8,128)S(1)} %compare_convert_fusion.5, ...), kind=kLoop, calls=%fused_computation.84.clone.1 | loop fusion | flops 103805952 | bytes 217088 | tf_op jit(solution)/shard_map/while/body/eval_jaxpr/reduce_sum | solution.py:91
  505.6 24.3 %multiply_reduce_fusion.4 = (f32[4,256]{1,0:T(4,128)S(1)}, f32[4,256]{1,0:T(4,128)S(1)}, f32[4,256]{1,0:T(4,128)S(1)}) fusion(f32[4,9,256]{2,1,0:T(8,128)S(1)} %copy.126, f32[4,256]{1,0:T(4,128)S(1)} %get-tuple-element.527, f32[4,256]{1,0:T(4,128)S(1)} %get-tuple-element.528, f32[4,9,256]{2,1,0:T(8,128)S(1)} %compare_convert_fusion.5, ...), kind=kLoop, calls=%fused_computation.84.clone.1 | loop fusion | flops 103805952 | bytes 217088 | tf_op jit(solution)/shard_map/while/body/eval_jaxpr/reduce_sum | solution.py:91
  534.7 24.3 %multiply_reduce_fusion.4 = (f32[4,256]{1,0:T(4,128)S(1)}, f32[4,256]{1,0:T(4,128)S(1)}, f32[4,256]{1,0:T(4,128)S(1)}) fusion(f32[4,9,256]{2,1,0:T(8,128)S(1)} %copy.126, f32[4,256]{1,0:T(4,128)S(1)} %get-tuple-element.527, f32[4,256]{1,0:T(4,128)S(1)} %get-tuple-element.528, f32[4,9,256]{2,1,0:T(8,128)S(1)} %compare_convert_fusion.5, ...), kind=kLoop, calls=%fused_computation.84.clone.1 | loop fusion | flops 103805952 | bytes 217088 | tf_op jit(solution)/shard_map/while/body/eval_jaxpr/reduce_sum | solution.py:91
  559.1 9.8 %all-to-all-start.8 = ((f32[128,1,1,2,256]{4,3,2,1,0:T(2,128)}), f32[128,1,1,2,256]{4,3,2,1,0:T(2,128)S(1)}, u32[]{:S(2)}, u32[]{:S(2)}) async-start(f32[128,1,1,2,256]{4,3,2,1,0:T(2,128)} %bitcast.85), calls=%async_computation.8 | async-start | bytes 524288 | tf_op jit(solution)/shard_map/all_to_all | solution.py:26
  572.0 7.7 %all-to-all-done.8 = f32[128,1,1,2,256]{4,3,2,1,0:T(2,128)S(1)} async-done(((f32[128,1,1,2,256]{4,3,2,1,0:T(2,128)}), f32[128,1,1,2,256]{4,3,2,1,0:T(2,128)S(1)}, u32[]{:S(2)}, u32[]{:S(2)}) %all-to-all-start.8) | async-done | bytes 262176 | tf_op jit(solution)/shard_map/all_to_all | solution.py:26
  587.4 13.5 %all-to-all-done.7 = f32[128,1,1,2,3,256]{5,3,4,2,1,0:T(2,128)S(1)} async-done(((f32[128,1,1,2,3,256]{5,3,4,2,1,0:T(2,128)}), f32[128,1,1,2,3,256]{5,3,4,2,1,0:T(2,128)S(1)}, u32[]{:S(2)}, u32[]{:S(2)}) %all-to-all-start.7) | async-done | bytes 786464 | tf_op jit(solution)/shard_map/all_to_all | solution.py:26
  (487 shorter events, 199.6 us)
Async XLA Ops:
  3.0 20.8 %all-to-all-start.1 = ((f32[128,1,1,2]{3,2,1,0:T(1,128)}), f32[128,1,1,2]{3,2,1,0:T(1,128)S(1)}, u32[]{:S(2)}, u32[]{:S(2)}) async-start(f32[128,1,1,2]{3,2,1,0:T(1,128)} %bitcast.38), calls=%async_computation.1 | async-start | bytes 131072 | tf_op jit(solution)/shard_map/all_to_all | solution.py:26
  23.8 21.2 %all-to-all-start.2 = ((f32[128,1,1,2,3,256]{5,3,4,2,1,0:T(2,128)}), f32[128,1,1,2,3,256]{5,3,4,2,1,0:T(2,128)S(1)}, u32[]{:S(2)}, u32[]{:S(2)}) async-start(f32[128,1,1,2,3,256]{5,3,4,2,1,0:T(2,128)} %copy.88), calls=%async_computation.2 | async-start | bytes 1572864 | tf_op jit(solution)/shard_map/all_to_all | solution.py:26
  44.9 14.4 %all-to-all-start.5 = ((f32[128,1,1,2]{3,2,1,0:T(1,128)}), f32[128,1,1,2]{3,2,1,0:T(1,128)S(1)}, u32[]{:S(2)}, u32[]{:S(2)}) async-start(f32[128,1,1,2]{3,2,1,0:T(1,128)} %bitcast.65), calls=%async_computation.5 | async-start | bytes 131072 | tf_op jit(solution)/shard_map/all_to_all | solution.py:26
  57.4 29.5 %collective-permute-start = (f32[1,1,1,32,3,256]{5,4,3,2,1,0:T(4,128)S(1)}, f32[1,1,1,32,3,256]{5,4,3,2,1,0:T(4,128)S(1)}, u32[]{:S(2)}, u32[]{:S(2)}) collective-permute-start(f32[1,1,1,32,3,256]{5,4,3,2,1,0:T(4,128)S(1)} %bitcast.216), channel_id=1, source_target_pairs={{0,1},{1,2},{2,3},{3,4},{4,5},{5,6},{6,7},{7,0},{8,9},{9,10},{10,1... | collective-permute-start | bytes 294920 | tf_op jit(solution)/shard_map/ppermute | solution.py:39
  59.3 30.9 %all-to-all-start.4 = ((f32[128,1,1,2,256]{4,3,2,1,0:T(2,128)}), f32[128,1,1,2,256]{4,3,2,1,0:T(2,128)S(1)}, u32[]{:S(2)}, u32[]{:S(2)}) async-start(f32[128,1,1,2,256]{4,3,2,1,0:T(2,128)} %bitcast.60), calls=%async_computation.4 | async-start | bytes 524288 | tf_op jit(solution)/shard_map/all_to_all | solution.py:26
  73.2 4.8 collective-permute-start.10
  76.5 5.0 collective-permute-start.6
  79.4 4.9 collective-permute-start.9
  81.5 15.1 %collective-permute-start.1 = (f32[1,1,1,32,3,256]{5,4,3,2,1,0:T(4,128)S(1)}, f32[1,1,1,32,3,256]{5,4,3,2,1,0:T(4,128)S(1)}, u32[]{:S(2)}, u32[]{:S(2)}) collective-permute-start(f32[1,1,1,32,3,256]{5,4,3,2,1,0:T(4,128)S(1)} %bitcast.217), channel_id=1, source_target_pairs={{0,8},{8,16},{16,24},{24,0},{1,9},{9,17},{17,25},{25,1},{2,10},{10... | collective-permute-start | bytes 294920 | tf_op jit(solution)/shard_map/ppermute | solution.py:39
  81.6 15.1 %collective-permute-start.2 = (f32[1,1,1,32,3,256]{5,4,3,2,1,0:T(4,128)S(1)}, f32[1,1,1,32,3,256]{5,4,3,2,1,0:T(4,128)S(1)}, u32[]{:S(2)}, u32[]{:S(2)}) collective-permute-start(f32[1,1,1,32,3,256]{5,4,3,2,1,0:T(4,128)S(1)} %bitcast.218), channel_id=1, source_target_pairs={{0,32},{32,64},{64,96},{96,0},{1,33},{33,65},{65,97},{97,1},{2,34}... | collective-permute-start | bytes 294920 | tf_op jit(solution)/shard_map/ppermute | solution.py:39
  82.7 14.0 %collective-permute-start.3 = (f32[1,1,1,32,3,256]{5,4,3,2,1,0:T(4,128)S(1)}, f32[1,1,1,32,3,256]{5,4,3,2,1,0:T(4,128)S(1)}, u32[]{:S(2)}, u32[]{:S(2)}) collective-permute-start(f32[1,1,1,32,3,256]{5,4,3,2,1,0:T(4,128)S(1)} %bitcast.219), channel_id=1, source_target_pairs={{32,0},{64,32},{96,64},{0,96},{33,1},{65,33},{97,65},{1,97},{34,2}... | collective-permute-start | bytes 294920 | tf_op jit(solution)/shard_map/ppermute | solution.py:40
  84.3 12.4 %collective-permute-start.4 = (f32[1,1,1,32,3,256]{5,4,3,2,1,0:T(4,128)S(1)}, f32[1,1,1,32,3,256]{5,4,3,2,1,0:T(4,128)S(1)}, u32[]{:S(2)}, u32[]{:S(2)}) collective-permute-start(f32[1,1,1,32,3,256]{5,4,3,2,1,0:T(4,128)S(1)} %bitcast.220), channel_id=1, source_target_pairs={{8,0},{16,8},{24,16},{0,24},{9,1},{17,9},{25,17},{1,25},{10,2},{18... | collective-permute-start | bytes 294920 | tf_op jit(solution)/shard_map/ppermute | solution.py:40
  86.9 9.8 %collective-permute-start.5 = (f32[1,1,1,32,3,256]{5,4,3,2,1,0:T(4,128)S(1)}, f32[1,1,1,32,3,256]{5,4,3,2,1,0:T(4,128)S(1)}, u32[]{:S(2)}, u32[]{:S(2)}) collective-permute-start(f32[1,1,1,32,3,256]{5,4,3,2,1,0:T(4,128)S(1)} %bitcast.221), channel_id=1, source_target_pairs={{1,0},{2,1},{3,2},{4,3},{5,4},{6,5},{7,6},{0,7},{9,8},{10,9},{11,1... | collective-permute-start | bytes 294920 | tf_op jit(solution)/shard_map/ppermute | solution.py:40
  90.2 219.6 %all-to-all-start.3 = ((f32[128,1,1,2,3,256]{5,3,4,2,1,0:T(2,128)}), f32[128,1,1,2,3,256]{5,3,4,2,1,0:T(2,128)S(1)}, u32[]{:S(2)}, u32[]{:S(2)}) async-start(f32[128,1,1,2,3,256]{5,3,4,2,1,0:T(2,128)} %copy.91), calls=%async_computation.3 | async-start | bytes 1572864 | tf_op jit(solution)/shard_map/all_to_all | solution.py:26
  300.3 7.5 %collective-permute-start.12 = (f32[1,1,1,32,256]{4,3,2,1,0:T(8,128)S(1)}, f32[1,1,1,32,256]{4,3,2,1,0:T(8,128)S(1)}, u32[]{:S(2)}, u32[]{:S(2)}) collective-permute-start(f32[1,1,1,32,256]{4,3,2,1,0:T(8,128)S(1)} %reshape_reshape.36), channel_id=1, source_target_pairs={{0,1},{1,2},{2,3},{3,4},{4,5},{5,6},{6,7},{7,0},{8,9},{9,10},{10,1... | collective-permute-start | bytes 98312 | tf_op jit(solution)/shard_map/ppermute | solution.py:39
  302.3 23.7 %collective-permute-start.13 = (f32[1,1,1,32,256]{4,3,2,1,0:T(8,128)S(1)}, f32[1,1,1,32,256]{4,3,2,1,0:T(8,128)S(1)}, u32[]{:S(2)}, u32[]{:S(2)}) collective-permute-start(f32[1,1,1,32,256]{4,3,2,1,0:T(8,128)S(1)} %reshape_reshape.36), channel_id=1, source_target_pairs={{0,8},{8,16},{16,24},{24,0},{1,9},{9,17},{17,25},{25,1},{2,10},{10... | collective-permute-start | bytes 98312 | tf_op jit(solution)/shard_map/ppermute | solution.py:39
  303.7 22.4 %collective-permute-start.14 = (f32[1,1,1,32,256]{4,3,2,1,0:T(8,128)S(1)}, f32[1,1,1,32,256]{4,3,2,1,0:T(8,128)S(1)}, u32[]{:S(2)}, u32[]{:S(2)}) collective-permute-start(f32[1,1,1,32,256]{4,3,2,1,0:T(8,128)S(1)} %reshape_reshape.36), channel_id=1, source_target_pairs={{0,32},{32,64},{64,96},{96,0},{1,33},{33,65},{65,97},{97,1},{2,34}... | collective-permute-start | bytes 98312 | tf_op jit(solution)/shard_map/ppermute | solution.py:39
  304.9 21.2 %collective-permute-start.15 = (f32[1,1,1,32,256]{4,3,2,1,0:T(8,128)S(1)}, f32[1,1,1,32,256]{4,3,2,1,0:T(8,128)S(1)}, u32[]{:S(2)}, u32[]{:S(2)}) collective-permute-start(f32[1,1,1,32,256]{4,3,2,1,0:T(8,128)S(1)} %reshape_reshape.36), channel_id=1, source_target_pairs={{32,0},{64,32},{96,64},{0,96},{33,1},{65,33},{97,65},{1,97},{34,2}... | collective-permute-start | bytes 98312 | tf_op jit(solution)/shard_map/ppermute | solution.py:40
  306.3 19.7 %collective-permute-start.16 = (f32[1,1,1,32,256]{4,3,2,1,0:T(8,128)S(1)}, f32[1,1,1,32,256]{4,3,2,1,0:T(8,128)S(1)}, u32[]{:S(2)}, u32[]{:S(2)}) collective-permute-start(f32[1,1,1,32,256]{4,3,2,1,0:T(8,128)S(1)} %reshape_reshape.36), channel_id=1, source_target_pairs={{8,0},{16,8},{24,16},{0,24},{9,1},{17,9},{25,17},{1,25},{10,2},{18... | collective-permute-start | bytes 98312 | tf_op jit(solution)/shard_map/ppermute | solution.py:40
  307.8 18.3 %collective-permute-start.17 = (f32[1,1,1,32,256]{4,3,2,1,0:T(8,128)S(1)}, f32[1,1,1,32,256]{4,3,2,1,0:T(8,128)S(1)}, u32[]{:S(2)}, u32[]{:S(2)}) collective-permute-start(f32[1,1,1,32,256]{4,3,2,1,0:T(8,128)S(1)} %reshape_reshape.36), channel_id=1, source_target_pairs={{1,0},{2,1},{3,2},{4,3},{5,4},{6,5},{7,6},{0,7},{9,8},{10,9},{11,1... | collective-permute-start | bytes 98312 | tf_op jit(solution)/shard_map/ppermute | solution.py:40
  309.8 249.3 %all-to-all-start = ((f32[128,1,1,2]{3,2,1,0:T(1,128)}), f32[128,1,1,2]{3,2,1,0:T(1,128)S(1)}, u32[]{:S(2)}, u32[]{:S(2)}) async-start(f32[128,1,1,2]{3,2,1,0:T(1,128)} %bitcast.32), calls=%async_computation | async-start | bytes 131072 | tf_op jit(solution)/shard_map/all_to_all | solution.py:26
  559.1 20.6 %all-to-all-start.8 = ((f32[128,1,1,2,256]{4,3,2,1,0:T(2,128)}), f32[128,1,1,2,256]{4,3,2,1,0:T(2,128)S(1)}, u32[]{:S(2)}, u32[]{:S(2)}) async-start(f32[128,1,1,2,256]{4,3,2,1,0:T(2,128)} %bitcast.85), calls=%async_computation.8 | async-start | bytes 524288 | tf_op jit(solution)/shard_map/all_to_all | solution.py:26
  579.7 21.1 %all-to-all-start.7 = ((f32[128,1,1,2,3,256]{5,3,4,2,1,0:T(2,128)}), f32[128,1,1,2,3,256]{5,3,4,2,1,0:T(2,128)S(1)}, u32[]{:S(2)}, u32[]{:S(2)}) async-start(f32[128,1,1,2,3,256]{5,3,4,2,1,0:T(2,128)} %copy.104), calls=%async_computation.7 | async-start | bytes 1572864 | tf_op jit(solution)/shard_map/all_to_all | solution.py:26
  600.8 21.2 %all-to-all-start.6 = ((f32[128,1,1,2,3,256]{5,3,4,2,1,0:T(2,128)}), f32[128,1,1,2,3,256]{5,3,4,2,1,0:T(2,128)S(1)}, u32[]{:S(2)}, u32[]{:S(2)}) async-start(f32[128,1,1,2,3,256]{5,3,4,2,1,0:T(2,128)} %copy.102), calls=%async_computation.6 | async-start | bytes 1572864 | tf_op jit(solution)/shard_map/all_to_all | solution.py:26
  (7 other events, 151.4 us)
where the time goes:
time: 632 us; the launch traced here: 630 us
  other arithmetic  372 us (59%)
  local copies, waits for them, and re-layouts  123 us (19%)
  starting transfers between devices  87.1 us (14%)
  waiting for transfers between devices  45.4 us (7%)
    reduce_sum x8, other arithmetic, accel_group(): jnp.sum(pair_weight * offsets[component], axis=(2, 3)) * scale_term  195 us
    reduce_sum x8, other arithmetic, density_group(): total = jnp.sum(kernel * weights, axis=(2, 3))  169 us
    all_to_all x9, starting transfers between devices, one_exchange(): parts = lax.all_to_all(parts, axis, split_axis=0, concat_axis=0, tiled=True)  60.6 us
    all_to_all x9, waiting for transfers between devices, one_exchange(): parts = lax.all_to_all(parts, axis, split_axis=0, concat_axis=0, tiled=True)  45.1 us
    scatter x7, local copies, waits for them, and re-layouts, relocate(): placed.append(holder.at[place_index].set(item, mode='drop'))  34.9 us
    gather x16, local copies, waits for them, and re-layouts, accel_step(): near_pos = jnp.concatenate([own_pos[:, None], table_pos[near_ids]], axis=1)  21.6 us
    gather x16, local copies, waits for them, and re-layouts, density_step(): near_pos = jnp.concatenate([own_pos[:, None], table_pos[near_ids]], axis=1)  21.6 us
    ppermute x9, starting transfers between devices, with_halo(): lax.ppermute(leading, axis, [(b, a) for a, b in up])  16.5 us
  transfers between devices with their start and end apart: 27, of which 6 were waited for; matrix products, arithmetic and copies ran while one was open for 77% of the time, Pallas kernels for 0%

commit v1 on v0

v1 whole, which is shorter than its diff:
```python
import functools
import math

import jax
import jax.numpy as jnp
from jax import lax
from jax.experimental import pallas as pl
from jax.experimental.pallas import tpu as pltpu
from jax.sharding import PartitionSpec as P

time_step = 0.1
LANES = 128
AXES = ("gx", "gy", "gz")

def split_up(array, dim, peers):
    before, after = (array.shape[:dim], array.shape[dim + 1 :])
    return jnp.moveaxis(array.reshape(*before, peers, -1, *after), dim, 0)


def joined_along(parts, dim):
    shape = list(parts.shape[1:])
    shape[dim] *= parts.shape[0]
    return jnp.moveaxis(parts, 0, dim).reshape(shape)


def one_exchange(array, axis, axes, splits, concats):
    sizes = [lax.axis_size(a) for a in axes]
    parts = split_up(array, splits[0], sizes[0])
    parts = jnp.moveaxis(split_up(parts, splits[1] + 1, sizes[1]), 0, 1)
    inside = parts.shape[2:]
    parts = parts.reshape(-1, *inside)
    parts = lax.all_to_all(parts, axis, split_axis=0, concat_axis=0, tiled=True)
    parts = joined_along(parts.reshape(*sizes, *inside), concats[0] + 1)
    return joined_along(parts, concats[1])


def relocate(fields, plan):
    cell_count = plan.shape[0]
    devices = lax.axis_size("gx") * lax.axis_size("gy") * lax.axis_size("gz")
    capacity = max(2, cell_count // devices)
    target = plan // cell_count
    ladder = jnp.arange(cell_count, dtype=jnp.int32)
    earlier = (target[:, None] == target[None, :]) & (ladder[None, :] < ladder[:, None])
    slot_rank = jnp.sum(earlier.astype(jnp.int32), axis=1)
    send_slot = target * capacity + slot_rank
    buffer_rows = devices * capacity
    arrival = (plan % cell_count).astype(jnp.float32)
    marker = jnp.full((buffer_rows,), -1.0, jnp.float32).at[send_slot].set(arrival)
    packed = tuple(
        (
            jnp.zeros((buffer_rows,) + field.shape[1:], jnp.float32).at[send_slot].set(field)
            for field in fields
        )
    ) + (marker,)
    count_x = lax.axis_size("gx")
    sectioned = tuple(
        (item.reshape((count_x, devices // count_x, capacity) + item.shape[1:]) for item in packed)
    )
    received = jax.tree.map(
        lambda part: one_exchange(part, ("gx", "gy", "gz"), ("gx", ("gy", "gz")), (0, 1), (0, 1)),
        sectioned,
    )
    flat = tuple(
        (item.reshape((buffer_rows,) + source.shape[1:]) for item, source in zip(received, packed))
    )
    landing = flat[-1]
    place_index = jnp.where(landing >= 0.0, landing, float(cell_count)).astype(jnp.int32)
    placed = []
    for item in flat[:-1]:
        holder = jnp.zeros((cell_count,) + item.shape[1:], jnp.float32)
        placed.append(holder.at[place_index].set(item, mode="drop"))
    return tuple(placed)


def neighbour_steps():
    return [(axis, step) for axis in AXES for step in (-1, 1)]


def halo_table(own):
    blocks = [own]
    for axis, step in neighbour_steps():
        peers = lax.axis_size(axis)
        blocks.append(lax.ppermute(own, axis, [((i + step) % peers, i) for i in range(peers)]))
    return jnp.concatenate(blocks, axis=0)


def near_table(neighbours, cell_count):
    sizes = {axis: lax.axis_size(axis) for axis in AXES}
    here = {axis: lax.axis_index(axis) for axis in AXES}
    owner = neighbours // cell_count
    block = jnp.zeros_like(owner)
    for number, (axis, step) in enumerate(neighbour_steps(), 1):
        there = dict(here)
        there[axis] = (here[axis] + step) % sizes[axis]
        device = (there["gx"] * sizes["gy"] + there["gy"]) * sizes["gz"] + there["gz"]
        block = jnp.where(owner == device, number, block)
    near = block * cell_count + neighbours % cell_count
    own = jnp.arange(cell_count, dtype=jnp.int32)[:, None]
    return jnp.concatenate([own, near], axis=1).reshape(-1)


def fixed_point(pos, box):
    parts = []
    for component in range(3):
        scaled = pos[:, component] * (2.0**32 / box[component])
        scaled = jnp.where(scaled >= 2.0**31, scaled - 2.0**32, scaled)
        parts.append(scaled.astype(jnp.int32))
    parts = jnp.stack(parts, axis=1)
    return jnp.pad(parts, ((0, 0), (0, 5), (0, 0)))


def gather_live(cell, near_ref, count_ref, pairs, partners):
    lane = lax.broadcasted_iota(jnp.int32, (8, LANES), 1)
    fill = jnp.int32(0)
    for partner in range(partners):
        b = near_ref[cell * partners + partner]
        live = count_ref[b]
        shift = fill & (LANES - 1)
        chunk = fill >> 7
        kept = lane < shift
        for table_ref, list_ref in pairs:
            first = pltpu.roll(table_ref[b, :, 0:LANES], shift, 1)
            second = pltpu.roll(table_ref[b, :, LANES : 2 * LANES], shift, 1)
            list_ref[chunk] = jnp.where(kept, list_ref[chunk], first)
            list_ref[chunk + 1] = jnp.where(kept, first, second)
            list_ref[chunk + 2] = second
        fill = fill + live
    return fill


def as_column(row):
    halves = []
    for half in range(2):
        part = row[:, half * LANES : (half + 1) * LANES]
        halves.append(jnp.broadcast_to(part, (LANES, LANES)).T)
    return halves


def store_column(ref, row):
    for half, block in enumerate(as_column(row)):
        ref[half * LANES : (half + 1) * LANES, :] = block


def row_sums(acc):
    ones = jnp.ones((8, LANES), jnp.float32)
    sums = lax.dot_general(
        ones, acc, (((1,), (1,)), ((), ())),
        precision=lax.Precision.HIGHEST, preferred_element_type=jnp.float32,
    )
    return sums[0:1, :]


def spread(list_ref, chunk, row):
    return jnp.broadcast_to(list_ref[chunk, row : row + 1, :], (8, LANES))


def offsets(i_refs, rows, others, shifts):
    parts = []
    for ref, other, shift in zip(i_refs, others, shifts):
        diff = ref[rows, :] - other
        if shift:
            diff = diff >> shift
        parts.append(diff.astype(jnp.float32))
    return parts


def density_kernel(partners, mass, unit, shifts, near_ref, count_ref, table_ref, h_ref, rho_ref,
                   list_ref, xi_ref, yi_ref, zi_ref, ci_ref, acc_ref):
    cells, particles = h_ref.shape[0], h_ref.shape[2]
    blocks = particles // 8
    i_refs = (xi_ref, yi_ref, zi_ref)
    lane = lax.broadcasted_iota(jnp.int32, (8, LANES), 1)
    factor = -math.log2(math.e) * unit * unit

    def one_cell(cell, carry):
        total = gather_live(cell, near_ref, count_ref, ((table_ref, list_ref),), partners)
        for component in range(3):
            store_column(i_refs[component], table_ref[cell, component : component + 1, :])
        h = h_ref[cell]
        store_column(ci_ref, factor / (h * h))
        last = (total - 1) >> 7

        def weights(chunk, others, block):
            rows = pl.ds(block * 8, 8)
            dx, dy, dz = offsets(i_refs, rows, others, shifts)
            return rows, jnp.exp2((dx * dx + dy * dy + dz * dz) * ci_ref[rows, :])

        others = [spread(list_ref, last, row) for row in range(3)]
        alive = lane < total - last * LANES
        for block in range(blocks):
            rows, w = weights(last, others, block)
            acc_ref[rows, :] = jnp.where(alive, w, 0.0)

        def one_chunk(chunk, inner):
            near = [spread(list_ref, chunk, row) for row in range(3)]
            for block in range(blocks):
                rows, w = weights(chunk, near, block)
                acc_ref[rows, :] += w
            return inner

        lax.fori_loop(0, last, one_chunk, 0)
        rho_ref[cell] = mass * (1.0 + row_sums(acc_ref[...])) / (h * h * h)
        return carry

    lax.fori_loop(0, cells, one_cell, 0)


def accel_kernel(partners, mass, unit, shifts, near_ref, count_ref, table_ref, inverse_ref, h_ref,
                 pos_ref, vel_ref, drifted_ref, kicked_ref,
                 list_ref, inverse_list_ref, xi_ref, yi_ref, zi_ref, ci_ref, ai_ref,
                 ax_ref, ay_ref, az_ref):
    cells, particles = h_ref.shape[0], h_ref.shape[2]
    blocks = particles // 8
    i_refs = (xi_ref, yi_ref, zi_ref)
    acc_refs = (ax_ref, ay_ref, az_ref)
    lane = lax.broadcasted_iota(jnp.int32, (8, LANES), 1)
    factor = -math.log2(math.e) * unit * unit

    def one_cell(cell, carry):
        total = gather_live(
            cell, near_ref, count_ref,
            ((table_ref, list_ref), (inverse_ref, inverse_list_ref)), partners,
        )
        for component in range(3):
            store_column(i_refs[component], table_ref[cell, component : component + 1, :])
        h = h_ref[cell]
        store_column(ci_ref, factor / (h * h))
        store_column(ai_ref, inverse_ref[cell, 0:1, :])
        last = (total - 1) >> 7

        def terms(others, other_inverse, block):
            rows = pl.ds(block * 8, 8)
            parts = offsets(i_refs, rows, others, shifts)
            dx, dy, dz = parts
            w = jnp.exp2((dx * dx + dy * dy + dz * dz) * ci_ref[rows, :])
            return rows, parts, w * (ai_ref[rows, :] + other_inverse)

        others = [spread(list_ref, last, row) for row in range(3)]
        other_inverse = spread(inverse_list_ref, last, 0)
        alive = lane < total - last * LANES
        for block in range(blocks):
            rows, parts, pair = terms(others, other_inverse, block)
            pair = jnp.where(alive, pair, 0.0)
            for acc_ref, part in zip(acc_refs, parts):
                acc_ref[rows, :] = pair * part

        def one_chunk(chunk, inner):
            near = [spread(list_ref, chunk, row) for row in range(3)]
            near_inverse = spread(inverse_list_ref, chunk, 0)
            for block in range(blocks):
                rows, parts, pair = terms(near, near_inverse, block)
                for acc_ref, part in zip(acc_refs, parts):
                    acc_ref[rows, :] += pair * part
            return inner

        lax.fori_loop(0, last, one_chunk, 0)
        scale = (time_step * 2.0 * mass * unit) / (h * h * h * h * h)
        for component, acc_ref in enumerate(acc_refs):
            row = slice(component, component + 1)
            kicked = vel_ref[cell, row, :] + row_sums(acc_ref[...]) * scale
            kicked_ref[cell, row, :] = kicked
            drifted_ref[cell, row, :] = pos_ref[cell, row, :] + time_step * kicked
        return carry

    lax.fori_loop(0, cells, one_cell, 0)


def shards(positions, smoothing, velocity, counts, plan_before, neighbours, plan_after):
    cell_count = positions.shape[0]
    particles = positions.shape[-1]
    partners = neighbours.shape[1] + 1
    box = (
        float(cell_count // 4 * lax.axis_size("gx")),
        float(2 * lax.axis_size("gy")),
        float(2 * lax.axis_size("gz")),
    )
    longest = max(box)
    shifts = tuple(int(round(math.log2(longest / length))) for length in box)
    unit = longest / 2.0**32
    mass = 1.0 / (partners * particles)
    placed_pos, placed_h, placed_vel, placed_count = relocate(
        (positions, smoothing, velocity, counts.astype(jnp.float32)), plan_before
    )
    near = near_table(neighbours, cell_count)
    table = fixed_point(halo_table(placed_pos), box)
    table_count = halo_table(placed_count).astype(jnp.int32)
    own_h = placed_h.reshape(cell_count, 1, particles)

    smem = pl.BlockSpec(memory_space=pltpu.SMEM)
    vmem = pl.BlockSpec(memory_space=pltpu.VMEM)
    chunks = partners * particles // LANES + 1
    square = (particles, LANES)
    columns = [pltpu.VMEM(square, jnp.int32)] * 3
    rho = pl.pallas_call(
        functools.partial(density_kernel, partners, mass, unit, shifts),
        out_shape=jax.ShapeDtypeStruct((cell_count, 1, particles), jnp.float32),
        in_specs=[smem, smem, vmem, vmem],
        out_specs=vmem,
        scratch_shapes=[pltpu.VMEM((chunks, 8, LANES), jnp.int32)] + columns
        + [pltpu.VMEM(square, jnp.float32)] * 2,
    )(near, table_count, table, own_h)

    inverse = 1.0 / halo_table(rho)
    inverse = jnp.broadcast_to(inverse, (inverse.shape[0], 8, particles))
    drifted, kicked = pl.pallas_call(
        functools.partial(accel_kernel, partners, mass, unit, shifts),
        out_shape=[jax.ShapeDtypeStruct(placed_pos.shape, jnp.float32)] * 2,
        in_specs=[smem, smem, vmem, vmem, vmem, vmem, vmem],
        out_specs=[vmem, vmem],
        scratch_shapes=[
            pltpu.VMEM((chunks, 8, LANES), jnp.int32),
            pltpu.VMEM((chunks, 8, LANES), jnp.float32),
        ]
        + columns
        + [pltpu.VMEM(square, jnp.float32)] * 5,
    )(near, table_count, table, inverse, own_h, placed_pos, placed_vel)
    final_pos, final_vel, final_rho = relocate(
        (drifted, kicked, rho.reshape(cell_count, particles)), plan_after
    )
    return (final_pos, final_vel, final_rho)


def solution(mesh):
    in_specs = (
        P(("gx", "gy", "gz"), None, None),
        P(("gx", "gy", "gz"), None),
        P(("gx", "gy", "gz"), None, None),
        P(("gx", "gy", "gz")),
        P(("gx", "gy", "gz")),
        P(("gx", "gy", "gz"), None),
        P(("gx", "gy", "gz")),
    )
    out_specs = (
        P(("gx", "gy", "gz"), None, None),
        P(("gx", "gy", "gz"), None, None),
        P(("gx", "gy", "gz"), None),
    )
    return jax.shard_map(shards, mesh=mesh, in_specs=in_specs, out_specs=out_specs, check_vma=False)
```

time: 632 us -> 323 us (0.51)
  other arithmetic: 372 us -> 4.26 us
  Pallas kernels: 0 us -> 102 us
  local copies, waits for them, and re-layouts: 123 us -> 66 us
  waiting for transfers between devices: 45.4 us -> 59.5 us
    reduce_sum x16 -> x0, other arithmetic: 363 us -> none  [the longest x8 195 us: accel_group(): jnp.sum(pair_weight * offsets[component], axis=(2, 3)) * scale_term]
    pallas_call x0 -> x2, Pallas kernels: none -> 102 us  [the longest x1 59.7 us: shards(): pl.pallas_call(functools.partial(accel_kernel, partners, mass, unit, shif...]
    gather x72 -> x0, local copies, waits for them, and re-layouts: 60.2 us -> none  [the longest x16 21.6 us: accel_step(): near_pos = jnp.concatenate([own_pos[:, None], table_pos[near_ids]], axis=1)]
    all_to_all x9, waiting for transfers between devices: 45.1 us -> 53.1 us  [one_exchange(): parts = lax.all_to_all(parts, axis, split_axis=0, concat_axis=0, tiled=True)]
  transfers between devices with their start and end apart: 27 -> 27, of which waited for: 6 -> 9; matrix products, arithmetic and copies ran while one was open for 77% -> 18% of each run, Pallas kernels for 0% -> 31%
where the time goes in v1:
time: 323 us
  Pallas kernels  102 us (32%)
  starting transfers between devices  90 us (28%)
  local copies, waits for them, and re-layouts  66 us (20%)
  waiting for transfers between devices  59.5 us (18%)
  other arithmetic  4.26 us (1%)
    all_to_all x9, starting transfers between devices, one_exchange(): parts = lax.all_to_all(parts, axis, split_axis=0, concat_axis=0, tiled=True)  65.3 us
    pallas_call x1, Pallas kernels, shards(): pl.pallas_call(functools.partial(accel_kernel, partners, mass, unit, shif...  59.7 us
    all_to_all x9, waiting for transfers between devices, one_exchange(): parts = lax.all_to_all(parts, axis, split_axis=0, concat_axis=0, tiled=True)  53.1 us
    pallas_call x1, Pallas kernels, shards(): pl.pallas_call(functools.partial(density_kernel, partners, mass, unit, sh...  41.8 us
    scatter x7, local copies, waits for them, and re-layouts, relocate(): placed.append(holder.at[place_index].set(item, mode='drop'))  34.9 us
    ppermute x18, starting transfers between devices, halo_table(): lax.ppermute(own, axis, [((i + step) % peers, i) for i in range(peers)])  24.7 us
    scatter x7, local copies, waits for them, and re-layouts, relocate(): jnp.zeros((buffer_rows,) + field.shape[1:], jnp.float32).at[send_slot]  9.7 us
    another operation x9, local copies, waits for them, and re-layouts, one_exchange(): parts = parts.reshape(-1, *inside)  9.19 us
  transfers between devices with their start and end apart: 27, of which 9 were waited for; matrix products, arithmetic and copies ran while one was open for 18% of the time, Pallas kernels for 31%

profile of v1, /device:TPU:1, one launch (start us, length us, event | category | flops | bytes accessed | tf_op | source)
XLA Modules:
  0.0 322.7 jit_solution(7412705983712760688)
XLA Ops:
  2.9 11.5 %all-to-all-start.1 = ((f32[128,1,1,2]{3,2,1,0:T(1,128)}), f32[128,1,1,2]{3,2,1,0:T(1,128)S(1)}, u32[]{:S(2)}, u32[]{:S(2)}) async-start(f32[128,1,1,2]{3,2,1,0:T(1,128)} %bitcast.6), calls=%async_computation.1 | async-start | bytes 131072 | tf_op jit(solution)/shard_map/all_to_all | solution.py:32
  16.5 7.2 %all-to-all-done.1 = f32[128,1,1,2]{3,2,1,0:T(1,128)S(1)} async-done(((f32[128,1,1,2]{3,2,1,0:T(1,128)}), f32[128,1,1,2]{3,2,1,0:T(1,128)S(1)}, u32[]{:S(2)}, u32[]{:S(2)}) %all-to-all-start.1) | async-done | bytes 1056 | tf_op jit(solution)/shard_map/all_to_all | solution.py:32
  23.7 4.8 %all-to-all-start.2 = ((f32[128,1,1,2]{3,2,1,0:T(1,128)}), f32[128,1,1,2]{3,2,1,0:T(1,128)S(1)}, u32[]{:S(2)}, u32[]{:S(2)}) async-start(f32[128,1,1,2]{3,2,1,0:T(1,128)} %bitcast.12), calls=%async_computation.2 | async-start | bytes 131072 | tf_op jit(solution)/shard_map/all_to_all | solution.py:32
  30.4 7.5 %all-to-all-done.2 = f32[128,1,1,2]{3,2,1,0:T(1,128)S(1)} async-done(((f32[128,1,1,2]{3,2,1,0:T(1,128)}), f32[128,1,1,2]{3,2,1,0:T(1,128)S(1)}, u32[]{:S(2)}, u32[]{:S(2)}) %all-to-all-start.2) | async-done | bytes 1056 | tf_op jit(solution)/shard_map/all_to_all | solution.py:32
  37.8 4.8 %all-to-all-start.4 = ((f32[128,1,1,2,256]{4,3,2,1,0:T(2,128)}), f32[128,1,1,2,256]{4,3,2,1,0:T(2,128)S(1)}, u32[]{:S(2)}, u32[]{:S(2)}) async-start(f32[128,1,1,2,256]{4,3,2,1,0:T(2,128)} %bitcast.23), calls=%async_computation.4 | async-start | bytes 524288 | tf_op jit(solution)/shard_map/all_to_all | solution.py:32
  46.5 6.9 %all-to-all-done.4 = f32[128,1,1,2,256]{4,3,2,1,0:T(2,128)S(1)} async-done(((f32[128,1,1,2,256]{4,3,2,1,0:T(2,128)}), f32[128,1,1,2,256]{4,3,2,1,0:T(2,128)S(1)}, u32[]{:S(2)}, u32[]{:S(2)}) %all-to-all-start.4) | async-done | bytes 262176 | tf_op jit(solution)/shard_map/all_to_all | solution.py:32
  53.4 4.7 %all-to-all-start.3 = ((f32[128,1,1,2,3,256]{5,3,4,2,1,0:T(2,128)}), f32[128,1,1,2,3,256]{5,3,4,2,1,0:T(2,128)S(1)}, u32[]{:S(2)}, u32[]{:S(2)}) async-start(f32[128,1,1,2,3,256]{5,3,4,2,1,0:T(2,128)} %copy.55), calls=%async_computation.3 | async-start | bytes 1572864 | tf_op jit(solution)/shard_map/all_to_all | solution.py:32
  62.1 12.5 %all-to-all-done.3 = f32[128,1,1,2,3,256]{5,3,4,2,1,0:T(2,128)S(1)} async-done(((f32[128,1,1,2,3,256]{5,3,4,2,1,0:T(2,128)}), f32[128,1,1,2,3,256]{5,3,4,2,1,0:T(2,128)S(1)}, u32[]{:S(2)}, u32[]{:S(2)}) %all-to-all-start.3) | async-done | bytes 786464 | tf_op jit(solution)/shard_map/all_to_all | solution.py:32
  74.5 4.6 %all-to-all-start.5 = ((f32[128,1,1,2,3,256]{5,3,4,2,1,0:T(2,128)}), f32[128,1,1,2,3,256]{5,3,4,2,1,0:T(2,128)S(1)}, u32[]{:S(2)}, u32[]{:S(2)}) async-start(f32[128,1,1,2,3,256]{5,3,4,2,1,0:T(2,128)} %copy.64), calls=%async_computation.5 | async-start | bytes 1572864 | tf_op jit(solution)/shard_map/all_to_all | solution.py:32
  88.1 2.9 collective-permute-start.4
  97.5 7.5 %scatter_fusion.1 = f32[32,3,256]{2,1,0:T(4,128)S(1)} fusion(f32[32,3,256]{2,1,0:T(4,128)S(1)} %broadcast.158.clone.1, s32[256]{0:T(256)S(1)} %bitcast.129, f32[256,3,256]{2,1,0:T(4,128)S(1)} %bitcast.116), kind=kCustom, calls=%fused_computation.5 | custom fusion | bytes 2360320 | tf_op jit(solution)/shard_map/scatter | solution.py:71
  105.1 2.7 collective-permute-start.7
  111.4 5.8 %all-to-all-start = ((f32[128,1,1,2]{3,2,1,0:T(1,128)}), f32[128,1,1,2]{3,2,1,0:T(1,128)S(1)}, u32[]{:S(2)}, u32[]{:S(2)}) async-start(f32[128,1,1,2]{3,2,1,0:T(1,128)} %bitcast), calls=%async_computation | async-start | bytes 131072 | tf_op jit(solution)/shard_map/all_to_all | solution.py:32
  117.4 7.5 %scatter_fusion.3 = f32[32,3,256]{2,1,0:T(4,128)S(1)} fusion(f32[32,3,256]{2,1,0:T(4,128)S(1)} %broadcast.158.clone.2, s32[256]{0:T(256)S(1)} %bitcast.130, f32[256,3,256]{2,1,0:T(4,128)S(1)} %bitcast.115), kind=kCustom, calls=%fused_computation.9 | custom fusion | bytes 2360320 | tf_op jit(solution)/shard_map/scatter | solution.py:71
  126.3 3.1 collective-permute-done.11
  132.7 41.8 %shard_map.94 = f32[32,1,256]{2,1,0:T(1,128)} custom-call(s32[288]{0:T(512)} %reshape.193.near_ref, s32[224]{0:T(256)} %convert_element_type.57.count_ref, s32[224,8,256]{2,1,0:T(8,128)} %pad.4.table_ref, f32[32,1,256]{2,1,0:T(1,128)} %reshape.202.h_ref), custom_call_target="tpu_custom_call" | custom-call | tf_op jit(solution)/shard_map/pallas_call | solution.py:294
  186.9 8.7 %all-to-all-start.8 = ((f32[128,1,1,2,256]{4,3,2,1,0:T(2,128)}), f32[128,1,1,2,256]{4,3,2,1,0:T(2,128)S(1)}, u32[]{:S(2)}, u32[]{:S(2)}) async-start(f32[128,1,1,2,256]{4,3,2,1,0:T(2,128)} %bitcast.51), calls=%async_computation.8 | async-start | bytes 524288 | tf_op jit(solution)/shard_map/all_to_all | solution.py:32
  197.0 59.7 %shard_map.95 = (f32[32,3,256]{2,1,0:T(4,128)}, f32[32,3,256]{2,1,0:T(4,128)}) custom-call(s32[288]{0:T(512)} %reshape.193.near_ref, s32[224]{0:T(256)} %convert_element_type.57.count_ref, s32[224,8,256]{2,1,0:T(8,128)} %pad.4.table_ref, f32[224,8,256]{2,1,0:T(8,128)} %broadcast_in_dim.66.inverse_ref, f32[32,1,256]{2,1,0:T(1,128)} %reshape.202.h_ref, ...), custom_call_target="tpu_custom_call" | custom-call | tf_op jit(solution)/shard_map/pallas_call | solution.py:305
  260.8 15.8 %all-to-all-start.7 = ((f32[128,1,1,2,3,256]{5,3,4,2,1,0:T(2,128)}), f32[128,1,1,2,3,256]{5,3,4,2,1,0:T(2,128)S(1)}, u32[]{:S(2)}, u32[]{:S(2)}) async-start(f32[128,1,1,2,3,256]{5,3,4,2,1,0:T(2,128)} %copy.68), calls=%async_computation.7 | async-start | bytes 1572864 | tf_op jit(solution)/shard_map/all_to_all | solution.py:32
  279.6 13.4 %all-to-all-done.7 = f32[128,1,1,2,3,256]{5,3,4,2,1,0:T(2,128)S(1)} async-done(((f32[128,1,1,2,3,256]{5,3,4,2,1,0:T(2,128)}), f32[128,1,1,2,3,256]{5,3,4,2,1,0:T(2,128)S(1)}, u32[]{:S(2)}, u32[]{:S(2)}) %all-to-all-start.7) | async-done | bytes 786464 | tf_op jit(solution)/shard_map/all_to_all | solution.py:32
  293.0 4.7 %all-to-all-start.6 = ((f32[128,1,1,2,3,256]{5,3,4,2,1,0:T(2,128)}), f32[128,1,1,2,3,256]{5,3,4,2,1,0:T(2,128)S(1)}, u32[]{:S(2)}, u32[]{:S(2)}) async-start(f32[128,1,1,2,3,256]{5,3,4,2,1,0:T(2,128)} %copy.66), calls=%async_computation.6 | async-start | bytes 1572864 | tf_op jit(solution)/shard_map/all_to_all | solution.py:32
  300.3 7.5 %scatter_fusion.7 = f32[32,3,256]{2,1,0:T(4,128)S(1)} fusion(f32[32,3,256]{2,1,0:T(4,128)S(1)} %broadcast.158.clone.3, s32[256]{0:T(256)S(1)} %bitcast.132, f32[256,3,256]{2,1,0:T(4,128)S(1)} %bitcast.117), kind=kCustom, calls=%fused_computation.13 | custom fusion | bytes 2360320 | tf_op jit(solution)/shard_map/scatter | solution.py:71
  308.5 5.7 %all-to-all-done.6 = f32[128,1,1,2,3,256]{5,3,4,2,1,0:T(2,128)S(1)} async-done(((f32[128,1,1,2,3,256]{5,3,4,2,1,0:T(2,128)}), f32[128,1,1,2,3,256]{5,3,4,2,1,0:T(2,128)S(1)}, u32[]{:S(2)}, u32[]{:S(2)}) %all-to-all-start.6) | async-done | bytes 786464 | tf_op jit(solution)/shard_map/all_to_all | solution.py:32
  314.5 7.5 %scatter_fusion.5 = f32[32,3,256]{2,1,0:T(4,128)S(1)} fusion(f32[32,3,256]{2,1,0:T(4,128)S(1)} %broadcast.158.clone, s32[256]{0:T(256)S(1)} %bitcast.133, f32[256,3,256]{2,1,0:T(4,128)S(1)} %bitcast.114), kind=kCustom, calls=%fused_computation.11 | custom fusion | bytes 2360320 | tf_op jit(solution)/shard_map/scatter | solution.py:71
  (127 shorter events, 62.6 us)
Async XLA Ops:
  2.9 20.8 %all-to-all-start.1 = ((f32[128,1,1,2]{3,2,1,0:T(1,128)}), f32[128,1,1,2]{3,2,1,0:T(1,128)S(1)}, u32[]{:S(2)}, u32[]{:S(2)}) async-start(f32[128,1,1,2]{3,2,1,0:T(1,128)} %bitcast.6), calls=%async_computation.1 | async-start | bytes 131072 | tf_op jit(solution)/shard_map/all_to_all | solution.py:32
  23.7 14.1 %all-to-all-start.2 = ((f32[128,1,1,2]{3,2,1,0:T(1,128)}), f32[128,1,1,2]{3,2,1,0:T(1,128)S(1)}, u32[]{:S(2)}, u32[]{:S(2)}) async-start(f32[128,1,1,2]{3,2,1,0:T(1,128)} %bitcast.12), calls=%async_computation.2 | async-start | bytes 131072 | tf_op jit(solution)/shard_map/all_to_all | solution.py:32
  37.8 15.6 %all-to-all-start.4 = ((f32[128,1,1,2,256]{4,3,2,1,0:T(2,128)}), f32[128,1,1,2,256]{4,3,2,1,0:T(2,128)S(1)}, u32[]{:S(2)}, u32[]{:S(2)}) async-start(f32[128,1,1,2,256]{4,3,2,1,0:T(2,128)} %bitcast.23), calls=%async_computation.4 | async-start | bytes 524288 | tf_op jit(solution)/shard_map/all_to_all | solution.py:32
  53.4 21.1 %all-to-all-start.3 = ((f32[128,1,1,2,3,256]{5,3,4,2,1,0:T(2,128)}), f32[128,1,1,2,3,256]{5,3,4,2,1,0:T(2,128)S(1)}, u32[]{:S(2)}, u32[]{:S(2)}) async-start(f32[128,1,1,2,3,256]{5,3,4,2,1,0:T(2,128)} %copy.55), calls=%async_computation.3 | async-start | bytes 1572864 | tf_op jit(solution)/shard_map/all_to_all | solution.py:32
  74.5 36.8 %all-to-all-start.5 = ((f32[128,1,1,2,3,256]{5,3,4,2,1,0:T(2,128)}), f32[128,1,1,2,3,256]{5,3,4,2,1,0:T(2,128)S(1)}, u32[]{:S(2)}, u32[]{:S(2)}) async-start(f32[128,1,1,2,3,256]{5,3,4,2,1,0:T(2,128)} %copy.64), calls=%async_computation.5 | async-start | bytes 1572864 | tf_op jit(solution)/shard_map/all_to_all | solution.py:32
  82.6 8.4 %collective-permute-start = (f32[32]{0:T(128)S(1)}, f32[32]{0:T(128)S(1)}, u32[]{:S(2)}, u32[]{:S(2)}) collective-permute-start(f32[32]{0:T(128)S(1)} %scatter_custom_fusion.3), channel_id=1, source_target_pairs={{96,0},{0,32},{32,64},{64,96},{97,1},{1,33},{33,65},{65,97},{98,2}... | collective-permute-start | bytes 392 | tf_op jit(solution)/shard_map/ppermute | solution.py:83
  84.0 7.0 %collective-permute-start.1 = (f32[32]{0:T(128)S(1)}, f32[32]{0:T(128)S(1)}, u32[]{:S(2)}, u32[]{:S(2)}) collective-permute-start(f32[32]{0:T(128)S(1)} %scatter_custom_fusion.3), channel_id=1, source_target_pairs={{32,0},{64,32},{96,64},{0,96},{33,1},{65,33},{97,65},{1,97},{34,2}... | collective-permute-start | bytes 392 | tf_op jit(solution)/shard_map/ppermute | solution.py:83
  85.3 5.7 %collective-permute-start.2 = (f32[32]{0:T(128)S(1)}, f32[32]{0:T(128)S(1)}, u32[]{:S(2)}, u32[]{:S(2)}) collective-permute-start(f32[32]{0:T(128)S(1)} %scatter_custom_fusion.3), channel_id=1, source_target_pairs={{24,0},{0,8},{8,16},{16,24},{25,1},{1,9},{9,17},{17,25},{26,2},{2,... | collective-permute-start | bytes 392 | tf_op jit(solution)/shard_map/ppermute | solution.py:83
  105.1 19.9 %collective-permute-start.6 = (f32[32,3,256]{2,1,0:T(4,128)S(1)}, f32[32,3,256]{2,1,0:T(4,128)S(1)}, u32[]{:S(2)}, u32[]{:S(2)}) collective-permute-start(f32[32,3,256]{2,1,0:T(4,128)S(1)} %scatter_fusion.1), channel_id=1, source_target_pairs={{96,0},{0,32},{32,64},{64,96},{97,1},{1,33},{33,65},{65,97},{98,2}... | collective-permute-start | bytes 294920 | tf_op jit(solution)/shard_map/ppermute | solution.py:83
  105.1 21.0 %collective-permute-start.7 = (f32[32,3,256]{2,1,0:T(4,128)S(1)}, f32[32,3,256]{2,1,0:T(4,128)S(1)}, u32[]{:S(2)}, u32[]{:S(2)}) collective-permute-start(f32[32,3,256]{2,1,0:T(4,128)S(1)} %scatter_fusion.1), channel_id=1, source_target_pairs={{32,0},{64,32},{96,64},{0,96},{33,1},{65,33},{97,65},{1,97},{34,2}... | collective-permute-start | bytes 294920 | tf_op jit(solution)/shard_map/ppermute | solution.py:83
  107.8 18.4 %collective-permute-start.8 = (f32[32,3,256]{2,1,0:T(4,128)S(1)}, f32[32,3,256]{2,1,0:T(4,128)S(1)}, u32[]{:S(2)}, u32[]{:S(2)}) collective-permute-start(f32[32,3,256]{2,1,0:T(4,128)S(1)} %scatter_fusion.1), channel_id=1, source_target_pairs={{24,0},{0,8},{8,16},{16,24},{25,1},{1,9},{9,17},{17,25},{26,2},{2,... | collective-permute-start | bytes 294920 | tf_op jit(solution)/shard_map/ppermute | solution.py:83
  108.6 17.7 %collective-permute-start.9 = (f32[32,3,256]{2,1,0:T(4,128)S(1)}, f32[32,3,256]{2,1,0:T(4,128)S(1)}, u32[]{:S(2)}, u32[]{:S(2)}) collective-permute-start(f32[32,3,256]{2,1,0:T(4,128)S(1)} %scatter_fusion.1), channel_id=1, source_target_pairs={{8,0},{16,8},{24,16},{0,24},{9,1},{17,9},{25,17},{1,25},{10,2},{18... | collective-permute-start | bytes 294920 | tf_op jit(solution)/shard_map/ppermute | solution.py:83
  110.5 15.8 %collective-permute-start.10 = (f32[32,3,256]{2,1,0:T(4,128)S(1)}, f32[32,3,256]{2,1,0:T(4,128)S(1)}, u32[]{:S(2)}, u32[]{:S(2)}) collective-permute-start(f32[32,3,256]{2,1,0:T(4,128)S(1)} %scatter_fusion.1), channel_id=1, source_target_pairs={{7,0},{0,1},{1,2},{2,3},{3,4},{4,5},{5,6},{6,7},{15,8},{8,9},{9,10... | collective-permute-start | bytes 294920 | tf_op jit(solution)/shard_map/ppermute | solution.py:83
  111.4 75.6 %all-to-all-start = ((f32[128,1,1,2]{3,2,1,0:T(1,128)}), f32[128,1,1,2]{3,2,1,0:T(1,128)S(1)}, u32[]{:S(2)}, u32[]{:S(2)}) async-start(f32[128,1,1,2]{3,2,1,0:T(1,128)} %bitcast), calls=%async_computation | async-start | bytes 131072 | tf_op jit(solution)/shard_map/all_to_all | solution.py:32
  125.0 4.4 %collective-permute-start.11 = (f32[32,3,256]{2,1,0:T(4,128)S(1)}, f32[32,3,256]{2,1,0:T(4,128)S(1)}, u32[]{:S(2)}, u32[]{:S(2)}) collective-permute-start(f32[32,3,256]{2,1,0:T(4,128)S(1)} %scatter_fusion.1), channel_id=1, source_target_pairs={{1,0},{2,1},{3,2},{4,3},{5,4},{6,5},{7,6},{0,7},{9,8},{10,9},{11,1... | collective-permute-start | bytes 294920 | tf_op jit(solution)/shard_map/ppermute | solution.py:83
  175.3 10.2 %collective-permute-start.12 = (f32[32,1,256]{2,0,1:T(8,128)S(1)}, f32[32,1,256]{2,0,1:T(8,128)S(1)}, u32[]{:S(2)}, u32[]{:S(2)}) collective-permute-start(f32[32,1,256]{2,0,1:T(8,128)S(1)} %copy.73), channel_id=1, source_target_pairs={{96,0},{0,32},{32,64},{64,96},{97,1},{1,33},{33,65},{65,97},{98,2}... | collective-permute-start | bytes 98312 | tf_op jit(solution)/shard_map/ppermute | solution.py:83
  178.2 8.7 %collective-permute-start.13 = (f32[32,1,256]{2,0,1:T(8,128)S(1)}, f32[32,1,256]{2,0,1:T(8,128)S(1)}, u32[]{:S(2)}, u32[]{:S(2)}) collective-permute-start(f32[32,1,256]{2,0,1:T(8,128)S(1)} %copy.73), channel_id=1, source_target_pairs={{32,0},{64,32},{96,64},{0,96},{33,1},{65,33},{97,65},{1,97},{34,2}... | collective-permute-start | bytes 98312 | tf_op jit(solution)/shard_map/ppermute | solution.py:83
  178.8 8.1 %collective-permute-start.14 = (f32[32,1,256]{2,0,1:T(8,128)S(1)}, f32[32,1,256]{2,0,1:T(8,128)S(1)}, u32[]{:S(2)}, u32[]{:S(2)}) collective-permute-start(f32[32,1,256]{2,0,1:T(8,128)S(1)} %copy.73), channel_id=1, source_target_pairs={{24,0},{0,8},{8,16},{16,24},{25,1},{1,9},{9,17},{17,25},{26,2},{2,... | collective-permute-start | bytes 98312 | tf_op jit(solution)/shard_map/ppermute | solution.py:83
  180.8 6.1 %collective-permute-start.15 = (f32[32,1,256]{2,0,1:T(8,128)S(1)}, f32[32,1,256]{2,0,1:T(8,128)S(1)}, u32[]{:S(2)}, u32[]{:S(2)}) collective-permute-start(f32[32,1,256]{2,0,1:T(8,128)S(1)} %copy.73), channel_id=1, source_target_pairs={{8,0},{16,8},{24,16},{0,24},{9,1},{17,9},{25,17},{1,25},{10,2},{18... | collective-permute-start | bytes 98312 | tf_op jit(solution)/shard_map/ppermute | solution.py:83
  181.6 5.2 %collective-permute-start.16 = (f32[32,1,256]{2,0,1:T(8,128)S(1)}, f32[32,1,256]{2,0,1:T(8,128)S(1)}, u32[]{:S(2)}, u32[]{:S(2)}) collective-permute-start(f32[32,1,256]{2,0,1:T(8,128)S(1)} %copy.73), channel_id=1, source_target_pairs={{7,0},{0,1},{1,2},{2,3},{3,4},{4,5},{5,6},{6,7},{15,8},{8,9},{9,10... | collective-permute-start | bytes 98312 | tf_op jit(solution)/shard_map/ppermute | solution.py:83
  185.5 10.1 %collective-permute-start.17 = (f32[32,1,256]{2,1,0:T(1,128)}, f32[32,1,256]{2,1,0:T(1,128)S(1)}, u32[]{:S(2)}, u32[]{:S(2)}) collective-permute-start(f32[32,1,256]{2,1,0:T(1,128)} %shard_map.94), channel_id=1, source_target_pairs={{1,0},{2,1},{3,2},{4,3},{5,4},{6,5},{7,6},{0,7},{9,8},{10,9},{11,1... | collective-permute-start | bytes 98312 | tf_op jit(solution)/shard_map/ppermute | solution.py:83
  186.9 73.9 %all-to-all-start.8 = ((f32[128,1,1,2,256]{4,3,2,1,0:T(2,128)}), f32[128,1,1,2,256]{4,3,2,1,0:T(2,128)S(1)}, u32[]{:S(2)}, u32[]{:S(2)}) async-start(f32[128,1,1,2,256]{4,3,2,1,0:T(2,128)} %bitcast.51), calls=%async_computation.8 | async-start | bytes 524288 | tf_op jit(solution)/shard_map/all_to_all | solution.py:32
  260.8 32.2 %all-to-all-start.7 = ((f32[128,1,1,2,3,256]{5,3,4,2,1,0:T(2,128)}), f32[128,1,1,2,3,256]{5,3,4,2,1,0:T(2,128)S(1)}, u32[]{:S(2)}, u32[]{:S(2)}) async-start(f32[128,1,1,2,3,256]{5,3,4,2,1,0:T(2,128)} %copy.68), calls=%async_computation.7 | async-start | bytes 1572864 | tf_op jit(solution)/shard_map/all_to_all | solution.py:32
  293.0 21.2 %all-to-all-start.6 = ((f32[128,1,1,2,3,256]{5,3,4,2,1,0:T(2,128)}), f32[128,1,1,2,3,256]{5,3,4,2,1,0:T(2,128)S(1)}, u32[]{:S(2)}, u32[]{:S(2)}) async-start(f32[128,1,1,2,3,256]{5,3,4,2,1,0:T(2,128)} %copy.66), calls=%async_computation.6 | async-start | bytes 1572864 | tf_op jit(solution)/shard_map/all_to_all | solution.py:32
  (9 other events, 101.7 us)

commit v2 on v1

v2 whole, which is shorter than its diff:
```python
import functools
import math

import jax
import jax.numpy as jnp
from jax import lax
from jax.experimental import pallas as pl
from jax.experimental.pallas import tpu as pltpu
from jax.sharding import PartitionSpec as P

time_step = 0.1
LANES = 128
AXES = ("gx", "gy", "gz")
MESH = pl.DeviceIdType.MESH

def neighbour_steps():
    return [(axis, step) for axis in AXES for step in (-1, 1)]


def slots_of(plan, cell_count, devices):
    target = plan // cell_count
    ladder = jnp.arange(cell_count, dtype=jnp.int32)
    earlier = (target[:, None] == target[None, :]) & (ladder[None, :] < ladder[:, None])
    rank = jnp.sum(earlier.astype(jnp.int32), axis=1)
    slot = target * 2 + rank
    every = jnp.arange(devices * 2, dtype=jnp.int32)
    cell = jnp.sum(jnp.where(slot[None, :] == every[:, None], ladder[None, :], 0), axis=1)
    return plan * 2 + rank, cell


def near_table(neighbours, cell_count):
    sizes = {axis: lax.axis_size(axis) for axis in AXES}
    here = {axis: lax.axis_index(axis) for axis in AXES}
    owner = neighbours // cell_count
    block = jnp.zeros_like(owner)
    for number, (axis, step) in enumerate(neighbour_steps(), 1):
        there = dict(here)
        there[axis] = (here[axis] + step) % sizes[axis]
        device = (there["gx"] * sizes["gy"] + there["gy"]) * sizes["gz"] + there["gz"]
        block = jnp.where(owner == device, number, block)
    near = block * cell_count + neighbours % cell_count
    own = jnp.arange(cell_count, dtype=jnp.int32)[:, None]
    return jnp.concatenate([own, near], axis=1).reshape(-1)


def exchange(sizes, pairs, send_sems, recv_sems):
    count_x, count_y, count_z = sizes
    devices = count_x * count_y * count_z
    here = [lax.axis_index(axis) for axis in AXES]
    me = (here[0] * count_y + here[1]) * count_z + here[2]

    def send(step, carry):
        there_x = lax.rem(here[0] + lax.div(step, count_y * count_z), count_x)
        there_y = lax.rem(here[1] + lax.rem(lax.div(step, count_z), count_y), count_y)
        there_z = lax.rem(here[2] + lax.rem(step, count_z), count_z)
        there = (there_x * count_y + there_y) * count_z + there_z
        for number, (source, target, whole) in enumerate(pairs):
            pltpu.make_async_remote_copy(
                src_ref=source if whole else source.at[there],
                dst_ref=target.at[me],
                send_sem=send_sems.at[number],
                recv_sem=recv_sems.at[number],
                device_id=(there_x, there_y, there_z),
                device_id_type=MESH,
            ).start()
        return carry

    lax.fori_loop(1, devices, send, 0)
    for source, target, whole in pairs:
        target[me] = source[...] if whole else source[me]
    for number, (source, target, whole) in enumerate(pairs):
        most = target.at[pl.ds(0, devices - 1)]
        arrived = pltpu.make_async_remote_copy(
            src_ref=most, dst_ref=most, send_sem=send_sems.at[number],
            recv_sem=recv_sems.at[number], device_id=tuple(here), device_id_type=MESH,
        )
        arrived.wait_send()
        arrived.wait_recv()


def fill_blocks(cell_ref, q_ref, v_ref, sendq_ref, sendv_ref):
    def one(d, carry):
        first, second = cell_ref[2 * d], cell_ref[2 * d + 1]
        sendq_ref[d, 0] = q_ref[first]
        sendq_ref[d, 1] = q_ref[second]
        low, high = v_ref[first], v_ref[second]
        sendv_ref[d, 0] = low[0:4]
        sendv_ref[d, 1, 0:2] = low[4:6]
        sendv_ref[d, 1, 2:4] = high[0:2]
        sendv_ref[d, 2] = high[2:6]
        return carry

    lax.fori_loop(0, sendq_ref.shape[0], one, 0)


def velocity_rows(recvv_ref, slot):
    block, odd = slot >> 1, (slot & 1) == 1
    first, middle, last = recvv_ref[block, 0], recvv_ref[block, 1], recvv_ref[block, 2]
    even_rows = jnp.concatenate([first, middle[0:2]], axis=0)
    odd_rows = jnp.concatenate([middle[2:4], last], axis=0)
    rows = jnp.where(odd, odd_rows, even_rows)
    return rows[0:3], rows[3:6]


def first_exchange_kernel(sizes, cell_ref, meta_ref, pos_ref, h_ref, vel_ref,
                          recvq_ref, recvv_ref, metas_ref,
                          q_ref, v_ref, sendq_ref, sendv_ref, send_sems, recv_sems):
    for cell in range(pos_ref.shape[0]):
        for half in range(2):
            lanes = slice(half * LANES, (half + 1) * LANES)
            q_ref[cell, 4 * half : 4 * half + 3] = pos_ref[cell, :, lanes]
            q_ref[cell, 4 * half + 3 : 4 * half + 4] = h_ref[cell : cell + 1, lanes]
            v_ref[cell, 3 * half : 3 * half + 3] = vel_ref[cell, :, lanes]
    fill_blocks(cell_ref, q_ref, v_ref, sendq_ref, sendv_ref)
    exchange(
        sizes,
        ((meta_ref, metas_ref, True), (sendq_ref, recvq_ref, False), (sendv_ref, recvv_ref, False)),
        send_sems, recv_sems,
    )


def last_exchange_kernel(sizes, cell_ref, q_ref, v_ref, recvq_ref, recvv_ref,
                         sendq_ref, sendv_ref, send_sems, recv_sems):
    fill_blocks(cell_ref, q_ref, v_ref, sendq_ref, sendv_ref)
    exchange(
        sizes, ((sendq_ref, recvq_ref, False), (sendv_ref, recvv_ref, False)), send_sems, recv_sems
    )


def halo(sizes, own, table_ref, send_sems, recv_sems):
    here = [lax.axis_index(axis) for axis in AXES]
    copies = []
    for number, (axis, step) in enumerate(neighbour_steps()):
        there = list(here)
        dim = AXES.index(axis)
        there[dim] = lax.rem(here[dim] + sizes[dim] - step, sizes[dim])
        copies.append(
            pltpu.make_async_remote_copy(
                src_ref=own, dst_ref=table_ref.at[number + 1], send_sem=send_sems.at[number],
                recv_sem=recv_sems.at[number], device_id=tuple(there), device_id_type=MESH,
            )
        )
        copies[-1].start()
    return copies


def cell_halo_kernel(sizes, slot_ref, recvq_ref, table_ref, send_sems, recv_sems):
    for place in range(table_ref.shape[1]):
        table_ref[0, place] = recvq_ref[slot_ref[place]]
    for copy in halo(sizes, table_ref.at[0], table_ref, send_sems, recv_sems):
        copy.wait()


def rho_halo_kernel(sizes, rho_ref, table_ref, send_sems, recv_sems):
    copies = halo(sizes, rho_ref, table_ref, send_sems, recv_sems)
    table_ref[0] = rho_ref[...]
    for copy in copies:
        copy.wait()


def unpack_kernel(slot_ref, recvq_ref, recvv_ref, pos_ref, vel_ref, rho_ref):
    for place in range(pos_ref.shape[0]):
        slot = slot_ref[place]
        rows = recvq_ref[slot]
        velocity = velocity_rows(recvv_ref, slot)
        for half in range(2):
            lanes = slice(half * LANES, (half + 1) * LANES)
            pos_ref[place, :, lanes] = rows[4 * half : 4 * half + 3]
            rho_ref[place : place + 1, lanes] = rows[4 * half + 3 : 4 * half + 4]
            vel_ref[place, :, lanes] = velocity[half]


def fixed_point(table_ref, fixed_ref, box):
    row = lax.broadcasted_iota(jnp.int32, (8, LANES), 0) & 3
    scale = jnp.full((8, LANES), 2.0**32 / box[2], jnp.float32)
    scale = jnp.where(row == 0, 2.0**32 / box[0], jnp.where(row == 1, 2.0**32 / box[1], scale))
    scale = jnp.where(row == 3, 1.0, scale)
    cells = table_ref.shape[1]

    def one(cell, carry):
        for block in range(table_ref.shape[0]):
            scaled = table_ref[block, cell] * scale
            scaled = jnp.where(scaled >= 2.0**31, scaled - 2.0**32, scaled)
            fixed_ref[block * cells + cell] = scaled.astype(jnp.int32)
        return carry

    lax.fori_loop(0, cells, one, 0)


def gather_live(cell, near_ref, count_ref, pairs, partners):
    fill = jnp.int32(0)
    for partner in range(partners):
        b = near_ref[cell * partners + partner]
        live = count_ref[b]
        shift = fill & (LANES - 1)
        chunk = fill >> 7
        for table_ref, list_ref in pairs:
            rows = list_ref.shape[1]
            kept = lax.broadcasted_iota(jnp.int32, (rows, LANES), 1) < shift
            rolled = pltpu.roll(table_ref[b], shift, 1)
            first, second = rolled[0:rows], rolled[rows : 2 * rows]
            list_ref[chunk] = jnp.where(kept, list_ref[chunk], first)
            list_ref[chunk + 1] = jnp.where(kept, first, second)
            list_ref[chunk + 2] = second
        fill = fill + live
    return fill


def store_column(ref, halves):
    for half, part in enumerate(halves):
        ref[half * LANES : (half + 1) * LANES, :] = jnp.broadcast_to(part, (LANES, LANES)).T


def halves_of(ref, cell, row):
    step = ref.shape[1] // 2
    return [ref[cell, row + half * step : row + half * step + 1, :] for half in range(2)]


def row_sums(acc):
    ones = jnp.ones((8, LANES), jnp.float32)
    sums = lax.dot_general(
        ones, acc, (((1,), (1,)), ((), ())),
        precision=lax.Precision.HIGHEST, preferred_element_type=jnp.float32,
    )
    return [sums[0:1, 0:LANES], sums[0:1, LANES : 2 * LANES]]


def spread(list_ref, chunk, row):
    return jnp.broadcast_to(list_ref[chunk, row : row + 1, :], (8, LANES))


def offsets(i_refs, rows, others, shifts):
    parts = []
    for ref, other, shift in zip(i_refs, others, shifts):
        diff = ref[rows, :] - other
        if shift:
            diff = diff >> shift
        parts.append(diff.astype(jnp.float32))
    return parts


def density_kernel(partners, mass, unit, shifts, box, near_ref, count_ref, table_ref, rho_ref,
                   fixed_ref, list_ref, xi_ref, yi_ref, zi_ref, ci_ref, acc_ref):
    cells, particles = table_ref.shape[1], 2 * LANES
    blocks = particles // 8
    i_refs = (xi_ref, yi_ref, zi_ref)
    lane = lax.broadcasted_iota(jnp.int32, (8, LANES), 1)
    factor = -math.log2(math.e) * unit * unit
    fixed_point(table_ref, fixed_ref, box)

    def one_cell(cell, carry):
        total = gather_live(cell, near_ref, count_ref, ((fixed_ref, list_ref),), partners)
        for component in range(3):
            store_column(i_refs[component], halves_of(fixed_ref, cell, component))
        h = halves_of(table_ref.at[0], cell, 3)
        store_column(ci_ref, [factor / (part * part) for part in h])
        last = (total - 1) >> 7

        def weights(chunk, others, block):
            rows = pl.ds(block * 8, 8)
            dx, dy, dz = offsets(i_refs, rows, others, shifts)
            return rows, jnp.exp2((dx * dx + dy * dy + dz * dz) * ci_ref[rows, :])

        others = [spread(list_ref, last, row) for row in range(3)]
        alive = lane < total - last * LANES
        for block in range(blocks):
            rows, w = weights(last, others, block)
            acc_ref[rows, :] = jnp.where(alive, w, 0.0)

        def one_chunk(chunk, inner):
            near = [spread(list_ref, chunk, row) for row in range(3)]
            for block in range(blocks):
                rows, w = weights(chunk, near, block)
                acc_ref[rows, :] += w
            return inner

        lax.fori_loop(0, last, one_chunk, 0)
        for half, (part, total_half) in enumerate(zip(h, row_sums(acc_ref[...]))):
            rho_ref[cell, half : half + 1] = mass * (1.0 + total_half) / (part * part * part)
        return carry

    lax.fori_loop(0, cells, one_cell, 0)


def accel_kernel(partners, mass, unit, shifts, box, near_ref, count_ref, slot_ref, table_ref, rho_ref,
                 recvv_ref, q_ref, v_ref,
                 fixed_ref, inverse_ref, list_ref, inverse_list_ref, xi_ref, yi_ref, zi_ref, ci_ref, ai_ref,
                 ax_ref, ay_ref, az_ref):
    cells, particles = table_ref.shape[1], 2 * LANES
    blocks = particles // 8
    i_refs = (xi_ref, yi_ref, zi_ref)
    acc_refs = (ax_ref, ay_ref, az_ref)
    lane = lax.broadcasted_iota(jnp.int32, (8, LANES), 1)
    factor = -math.log2(math.e) * unit * unit
    fixed_point(table_ref, fixed_ref, box)

    def invert(cell, carry):
        for block in range(rho_ref.shape[0]):
            inverse_ref[block * cells + cell] = 1.0 / rho_ref[block, cell]
        return carry

    lax.fori_loop(0, cells, invert, 0)

    def one_cell(cell, carry):
        total = gather_live(
            cell, near_ref, count_ref,
            ((fixed_ref, list_ref), (inverse_ref, inverse_list_ref)), partners,
        )
        for component in range(3):
            store_column(i_refs[component], halves_of(fixed_ref, cell, component))
        h = halves_of(table_ref.at[0], cell, 3)
        store_column(ci_ref, [factor / (part * part) for part in h])
        store_column(ai_ref, halves_of(inverse_ref, cell, 0))
        last = (total - 1) >> 7

        def terms(others, other_inverse, block):
            rows = pl.ds(block * 8, 8)
            parts = offsets(i_refs, rows, others, shifts)
            dx, dy, dz = parts
            w = jnp.exp2((dx * dx + dy * dy + dz * dz) * ci_ref[rows, :])
            return rows, parts, w * (ai_ref[rows, :] + other_inverse)

        others = [spread(list_ref, last, row) for row in range(3)]
        other_inverse = spread(inverse_list_ref, last, 0)
        alive = lane < total - last * LANES
        for block in range(blocks):
            rows, parts, pair = terms(others, other_inverse, block)
            pair = jnp.where(alive, pair, 0.0)
            for acc_ref, part in zip(acc_refs, parts):
                acc_ref[rows, :] = pair * part

        def one_chunk(chunk, inner):
            near = [spread(list_ref, chunk, row) for row in range(3)]
            near_inverse = spread(inverse_list_ref, chunk, 0)
            for block in range(blocks):
                rows, parts, pair = terms(near, near_inverse, block)
                for acc_ref, part in zip(acc_refs, parts):
                    acc_ref[rows, :] += pair * part
            return inner

        lax.fori_loop(0, last, one_chunk, 0)
        scale = [(time_step * 2.0 * mass * unit) / (part * part * part * part * part) for part in h]
        velocity = velocity_rows(recvv_ref, slot_ref[cell])
        for component, acc_ref in enumerate(acc_refs):
            sums = row_sums(acc_ref[...])
            for half in range(2):
                kicked = velocity[half][component : component + 1] + sums[half] * scale[half]
                v_ref[cell, 3 * half + component : 3 * half + component + 1] = kicked
                row = slice(4 * half + component, 4 * half + component + 1)
                q_ref[cell, row] = table_ref[0, cell, row] + time_step * kicked
        for half in range(2):
            row = slice(4 * half + 3, 4 * half + 4)
            q_ref[cell, row] = rho_ref[0, cell, half : half + 1]
        return carry

    lax.fori_loop(0, cells, one_cell, 0)


def shards(positions, smoothing, velocity, counts, plan_before, neighbours, plan_after):
    cell_count = positions.shape[0]
    particles = positions.shape[-1]
    partners = neighbours.shape[1] + 1
    sizes = tuple(lax.axis_size(axis) for axis in AXES)
    devices = sizes[0] * sizes[1] * sizes[2]
    box = (float(cell_count // 4 * sizes[0]), float(2 * sizes[1]), float(2 * sizes[2]))
    longest = max(box)
    shifts = tuple(int(round(math.log2(longest / length))) for length in box)
    unit = longest / 2.0**32
    mass = 1.0 / (partners * particles)

    smem = pl.BlockSpec(memory_space=pltpu.SMEM)
    vmem = pl.BlockSpec(memory_space=pltpu.VMEM)
    f32 = lambda *shape: jax.ShapeDtypeStruct(shape, jnp.float32)
    effects = pltpu.CompilerParams(has_side_effects=True)
    sems = lambda count: [pltpu.SemaphoreType.DMA((count,))] * 2
    blocks_q, blocks_v = (devices, 2, 8, LANES), (devices, 3, 4, LANES)
    sends = [pltpu.VMEM(blocks_q, jnp.float32), pltpu.VMEM(blocks_v, jnp.float32)]
    cells8 = pltpu.VMEM((cell_count, 8, LANES), jnp.float32)

    key_before, cell_before = slots_of(plan_before, cell_count, devices)
    key_after, cell_after = slots_of(plan_after, cell_count, devices)
    meta = jnp.concatenate([key_before, key_after, counts, jnp.zeros_like(counts)])[None, :]
    recv_q, recv_v, metas = pl.pallas_call(
        functools.partial(first_exchange_kernel, sizes),
        out_shape=[f32(*blocks_q), f32(*blocks_v), jax.ShapeDtypeStruct((devices, 1, LANES), jnp.int32)],
        in_specs=[smem, vmem, vmem, vmem, vmem],
        out_specs=[vmem] * 3,
        scratch_shapes=[cells8, cells8] + sends + sems(3),
        compiler_params=effects,
        name="first_exchange",
    )(cell_before, meta, positions, smoothing, velocity)

    here = [lax.axis_index(axis) for axis in AXES]
    blocks = [tuple(here)]
    for axis, step in neighbour_steps():
        there = list(here)
        dim = AXES.index(axis)
        there[dim] = (here[dim] + step) % sizes[dim]
        blocks.append(tuple(there))
    first_place = jnp.stack([((x * sizes[1] + y) * sizes[2] + z) * cell_count for x, y, z in blocks])
    local = jnp.arange(cell_count, dtype=jnp.int32)
    place = (first_place[:, None] + local[None, :]).reshape(-1)
    keys, keys_after = metas[:, 0, 0:cell_count], metas[:, 0, cell_count : 2 * cell_count]
    all_counts = metas[:, 0, 2 * cell_count : 3 * cell_count]
    source = 2 * jnp.arange(devices, dtype=jnp.int32)[None, :, None]

    def pick(keys, places, values):
        hit = (keys >> 1)[None] == places[:, None, None]
        return jnp.sum(jnp.where(hit, values, 0), axis=(1, 2))

    own_place = place[:cell_count]
    table_count = pick(keys, place, all_counts[None])
    slot_before = pick(keys, own_place, (keys & 1)[None] + source)
    slot_after = pick(keys_after, own_place, (keys_after & 1)[None] + source)
    near = near_table(neighbours, cell_count)

    table = pl.pallas_call(
        functools.partial(cell_halo_kernel, sizes),
        out_shape=f32(7, cell_count, 8, LANES),
        in_specs=[smem, vmem],
        out_specs=vmem,
        scratch_shapes=sems(6),
        compiler_params=effects,
        name="cell_halo",
    )(slot_before, recv_q.reshape(2 * devices, 8, LANES))

    chunks = partners * particles // LANES + 1
    square = (particles, LANES)
    columns = [pltpu.VMEM(square, jnp.int32)] * 3
    fixed = pltpu.VMEM((7 * cell_count, 8, LANES), jnp.int32)
    rho = pl.pallas_call(
        functools.partial(density_kernel, partners, mass, unit, shifts, box),
        out_shape=f32(cell_count, 2, LANES),
        in_specs=[smem, smem, vmem],
        out_specs=vmem,
        scratch_shapes=[fixed, pltpu.VMEM((chunks, 4, LANES), jnp.int32)] + columns
        + [pltpu.VMEM(square, jnp.float32)] * 2,
        name="density",
    )(near, table_count, table)

    table_rho = pl.pallas_call(
        functools.partial(rho_halo_kernel, sizes),
        out_shape=f32(7, cell_count, 2, LANES),
        in_specs=[vmem],
        out_specs=vmem,
        scratch_shapes=sems(6),
        compiler_params=effects,
        name="rho_halo",
    )(rho)

    out_q, out_v = pl.pallas_call(
        functools.partial(accel_kernel, partners, mass, unit, shifts, box),
        out_shape=[f32(cell_count, 8, LANES)] * 2,
        in_specs=[smem, smem, smem, vmem, vmem, vmem],
        out_specs=[vmem, vmem],
        scratch_shapes=[
            fixed,
            pltpu.VMEM((7 * cell_count, 2, LANES), jnp.float32),
            pltpu.VMEM((chunks, 4, LANES), jnp.int32),
            pltpu.VMEM((chunks, 1, LANES), jnp.float32),
        ]
        + columns
        + [pltpu.VMEM(square, jnp.float32)] * 5,
        name="accel",
    )(near, table_count, slot_before, table, table_rho, recv_v)

    last_q, last_v = pl.pallas_call(
        functools.partial(last_exchange_kernel, sizes),
        out_shape=[f32(*blocks_q), f32(*blocks_v)],
        in_specs=[smem, vmem, vmem],
        out_specs=[vmem] * 2,
        scratch_shapes=sends + sems(2),
        compiler_params=effects,
        name="last_exchange",
    )(cell_after, out_q, out_v)
    return pl.pallas_call(
        unpack_kernel,
        out_shape=[f32(*positions.shape), f32(*velocity.shape), f32(*smoothing.shape)],
        in_specs=[smem, vmem, vmem],
        out_specs=[vmem] * 3,
        name="unpack",
    )(slot_after, last_q.reshape(2 * devices, 8, LANES), last_v)


def solution(mesh):
    in_specs = (
        P(("gx", "gy", "gz"), None, None),
        P(("gx", "gy", "gz"), None),
        P(("gx", "gy", "gz"), None, None),
        P(("gx", "gy", "gz")),
        P(("gx", "gy", "gz")),
        P(("gx", "gy", "gz"), None),
        P(("gx", "gy", "gz")),
    )
    out_specs = (
        P(("gx", "gy", "gz"), None, None),
        P(("gx", "gy", "gz"), None, None),
        P(("gx", "gy", "gz"), None),
    )
    return jax.shard_map(shards, mesh=mesh, in_specs=in_specs, out_specs=out_specs, check_vma=False)
```

time: 323 us -> 255 us (0.79)
  Pallas kernels: 102 us -> 230 us
  starting transfers between devices: 90 us -> 0 us
  waiting for transfers between devices: 59.5 us -> 0 us
  local copies, waits for them, and re-layouts: 66 us -> 7.59 us
  other arithmetic: 4.26 us -> 15.8 us
    pallas_call x0 -> x5, Pallas kernels: none -> 128 us  [the longest x1 49.4 us: shards(): pl.pallas_call(functools.partial(first_exchange_kernel, sizes), out_shape...]
    all_to_all x9 -> x0, starting transfers between devices: 65.3 us -> none  [one_exchange(): parts = lax.all_to_all(parts, axis, split_axis=0, concat_axis=0, tiled=True)]
    all_to_all x9 -> x0, waiting for transfers between devices: 53.1 us -> none  [one_exchange(): parts = lax.all_to_all(parts, axis, split_axis=0, concat_axis=0, tiled=True)]
    scatter x16 -> x0, local copies, waits for them, and re-layouts: 45.9 us -> none  [the longest x7 34.9 us: relocate(): placed.append(holder.at[place_index].set(item, mode='drop'))]
    ppermute x18 -> x0, starting transfers between devices: 24.7 us -> none  [halo_table(): lax.ppermute(own, axis, [((i + step) % peers, i) for i in range(peers)])]
    another operation x22 -> x3, local copies, waits for them, and re-layouts: 10.6 us -> 0.09 us  [the longest x1 0.09 us: shards(): jnp.stack([((x * sizes[1] + y) * sizes[2] + z) * cell_count for x, y, z i...]
    reduce_sum x2 -> x6, other arithmetic: 0.36 us -> 8.56 us  [the longest x2 6.9 us: pick(): return jnp.sum(jnp.where(hit, values, 0), axis=(1, 2))]
    ppermute x18 -> x0, waiting for transfers between devices: 6.4 us -> none  [halo_table(): lax.ppermute(own, axis, [((i + step) % peers, i) for i in range(peers)])]
  transfers between devices with their start and end apart: 27 -> 0, of which waited for: 9 -> 0; matrix products, arithmetic and copies ran while one was open for 18% -> 0% of each run, Pallas kernels for 31% -> 0%
where the time goes in v2:
time: 255 us
  Pallas kernels  230 us (90%)
  other arithmetic  15.8 us (6%)
  local copies, waits for them, and re-layouts  7.59 us (3%)
    pallas_call x1, Pallas kernels, shards(): pl.pallas_call(functools.partial(accel_kernel, partners, mass, unit, shif...  59.8 us
    pallas_call x1, Pallas kernels, shards(): pl.pallas_call(functools.partial(first_exchange_kernel, sizes), out_shape...  49.4 us
    pallas_call x1, Pallas kernels, shards(): pl.pallas_call(functools.partial(last_exchange_kernel, sizes), out_shape=...  48.9 us
    pallas_call x1, Pallas kernels, shards(): pl.pallas_call(functools.partial(density_kernel, partners, mass, unit, sh...  42.2 us
    pallas_call x1, Pallas kernels, shards(): pl.pallas_call(functools.partial(rho_halo_kernel, sizes), out_shape=f32(7...  15.6 us
    pallas_call x1, Pallas kernels, shards(): pl.pallas_call(functools.partial(cell_halo_kernel, sizes), out_shape=f32(...  12.2 us
    reduce_sum x2, other arithmetic, pick(): return jnp.sum(jnp.where(hit, values, 0), axis=(1, 2))  6.9 us

profile of v2, /device:TPU:1, one launch (start us, length us, event | category | flops | bytes accessed | tf_op | source)
XLA Modules:
  0.0 254.5 jit_solution(12057033709104220978)
XLA Ops:
  0.8 0.7 and_select_fusion.1
  1.7 0.7 and_select_fusion
  2.5 0.7 fusion.2
  3.2 0.7 multiply_add_fusion
  3.9 1.3 add_bitcast_fusion.meta_ref
  5.3 0.6 select_reduce_fusion.3.cell_ref
  5.9 0.6 select_reduce_fusion.4.cell_ref
  6.8 0.7 reshape.104.near_ref
  7.5 1.6 copy.25.pos_ref
  9.1 1.6 copy.26.vel_ref
  10.7 49.4 %first_exchange.1 = (f32[128,2,8,128]{3,2,1,0:T(8,128)}, f32[128,3,4,128]{3,2,1,0:T(4,128)}, s32[128,1,128]{2,1,0:T(1,128)}) custom-call(s32[256]{0:T(256)} %select_reduce_fusion.4.cell_ref, s32[1,128]{1,0:T(1,128)} %add_bitcast_fusion.meta_ref, f32[32,3,256]{2,1,0:T(4,128)} %copy.25.pos_ref, f32[32,256]{1,0:T(8,128)} %h_ref.1, f32[32,3,256]{2,1,0:T(4,128)} %copy.26.vel_ref), custom_call_target="tpu_custom_call" | custom-call | tf_op jit(solution)/shard_map/first_exchange/pallas_call | solution.py:383
  60.1 0.9 shift-right-arithmetic_bitcast_fusion.1
  61.1 1.2 fusion.4
  62.3 1.0 bitcast_add_fusion
  63.5 1.9 select_reduce_fusion.1
  65.4 5.0 %select_reduce_fusion.count_ref = s32[224]{0:T(256)} fusion(s32[128,32]{0,1:T(8,128)S(1)} %copy.33, s32[128,32]{0,1:T(8,128)S(1)} %copy.32, s32[224]{0:T(256)S(1)} %add.204), kind=kLoop, calls=%fused_computation | loop fusion | flops 2752288 | bytes 34560 | tf_op jit(solution)/shard_map/reduce_sum | solution.py:409
  70.4 12.2 %cell_halo.1.table_ref = f32[7,32,8,128]{3,2,1,0:T(8,128)} custom-call(s32[32]{0:T(128)} %get-tuple-element.26.slot_ref, f32[256,8,128]{2,1,0:T(8,128)} %bitcast.26), custom_call_target="tpu_custom_call" | custom-call | tf_op jit(solution)/shard_map/cell_halo/pallas_call | solution.py:417
  82.6 42.2 %density.1.rho_ref = f32[32,2,128]{2,1,0:T(2,128)} custom-call(s32[288]{0:T(512)} %reshape.104.near_ref, s32[224]{0:T(256)} %select_reduce_fusion.count_ref, f32[7,32,8,128]{3,2,1,0:T(8,128)} %cell_halo.1.table_ref), custom_call_target="tpu_custom_call" | custom-call | tf_op jit(solution)/shard_map/density/pallas_call | solution.py:431
  124.8 15.6 %rho_halo.1.rho_ref = f32[7,32,2,128]{3,2,1,0:T(2,128)} custom-call(f32[32,2,128]{2,1,0:T(2,128)} %density.1.rho_ref), custom_call_target="tpu_custom_call" | custom-call | tf_op jit(solution)/shard_map/rho_halo/pallas_call | solution.py:441
  140.3 59.8 %accel.1 = (f32[32,8,128]{2,1,0:T(8,128)}, f32[32,8,128]{2,1,0:T(8,128)}) custom-call(s32[288]{0:T(512)} %reshape.104.near_ref, s32[224]{0:T(256)} %select_reduce_fusion.count_ref, s32[32]{0:T(128)} %get-tuple-element.26.slot_ref, f32[7,32,8,128]{3,2,1,0:T(8,128)} %cell_halo.1.table_ref, f32[7,32,2,128]{3,2,1,0:T(2,128)} %rho_halo.1.rho_ref, ...), custom_call_target="tpu_custom_call" | custom-call | tf_op jit(solution)/shard_map/accel/pallas_call | solution.py:451
  200.2 48.9 %last_exchange.1 = (f32[128,2,8,128]{3,2,1,0:T(8,128)}, f32[128,3,4,128]{3,2,1,0:T(4,128)}) custom-call(s32[256]{0:T(256)} %select_reduce_fusion.3.cell_ref, f32[32,8,128]{2,1,0:T(8,128)} %get-tuple-element.13.q_ref, f32[32,8,128]{2,1,0:T(8,128)} %get-tuple-element.14.v_ref), custom_call_target="tpu_custom_call" | custom-call | tf_op jit(solution)/shard_map/last_exchange/pallas_call | solution.py:467
  249.1 2.3 unpack.1
  251.4 1.6 copy.37
  253.0 1.6 copy.38
  (18 shorter events, 1.0 us)

commit v3 on v2

--- a/solution.py
+++ b/solution.py
@@ -17,15 +17,15 @@
     return [(axis, step) for axis in AXES for step in (-1, 1)]
 
 
-def slots_of(plan, cell_count, devices):
-    target = plan // cell_count
+def slots_of(plans, cell_count, devices):
+    target = plans // cell_count
     ladder = jnp.arange(cell_count, dtype=jnp.int32)
-    earlier = (target[:, None] == target[None, :]) & (ladder[None, :] < ladder[:, None])
-    rank = jnp.sum(earlier.astype(jnp.int32), axis=1)
+    earlier = (target[:, :, None] == target[:, None, :]) & (ladder[None, :] < ladder[:, None])
+    rank = jnp.sum(earlier.astype(jnp.int32), axis=2)
     slot = target * 2 + rank
     every = jnp.arange(devices * 2, dtype=jnp.int32)
-    cell = jnp.sum(jnp.where(slot[None, :] == every[:, None], ladder[None, :], 0), axis=1)
-    return plan * 2 + rank, cell
+    hit = slot[:, None, :] == every[None, :, None]
+    return plans * 2 + rank, jnp.sum(jnp.where(hit, ladder, 0), axis=2)
 
 
 def near_table(neighbours, cell_count):
@@ -43,33 +43,54 @@
     return jnp.concatenate([own, near], axis=1).reshape(-1)
 
 
-def exchange(sizes, pairs, send_sems, recv_sems):
+def peer_offsets(sizes):
     count_x, count_y, count_z = sizes
-    devices = count_x * count_y * count_z
+    steps = [(x, y, z) for x in range(count_x) for y in range(count_y) for z in range(count_z)][1:]
+
+    def hops(step):
+        x, y, z = step
+        chips = count_z // 2
+        return min(x, count_x - x) + min(y, count_y - y) + min(z // 2, chips - z // 2)
+
+    return sorted(steps, key=lambda step: -hops(step))
+
+
+def shifted(here, step, sizes):
+    return tuple(lax.rem(h + d, n) if d else h for h, d, n in zip(here, step, sizes))
+
+
+def flat(place, sizes):
+    return (place[0] * sizes[1] + place[1]) * sizes[2] + place[2]
+
+
+def greet(peers):
+    barrier = pltpu.get_barrier_semaphore()
+    for peer in peers:
+        pl.semaphore_signal(barrier, inc=1, device_id=peer, device_id_type=MESH)
+    return barrier, len(peers)
+
+
+def exchange(sizes, fill, pairs, send_sems, recv_sems):
     here = [lax.axis_index(axis) for axis in AXES]
-    me = (here[0] * count_y + here[1]) * count_z + here[2]
-
-    def send(step, carry):
-        there_x = lax.rem(here[0] + lax.div(step, count_y * count_z), count_x)
-        there_y = lax.rem(here[1] + lax.rem(lax.div(step, count_z), count_y), count_y)
-        there_z = lax.rem(here[2] + lax.rem(step, count_z), count_z)
-        there = (there_x * count_y + there_y) * count_z + there_z
-        for number, (source, target, whole) in enumerate(pairs):
+    me = flat(here, sizes)
+    peers = [shifted(here, step, sizes) for step in peer_offsets(sizes)]
+    barrier, signals = greet(peers)
+    fill()
+    pl.semaphore_wait(barrier, signals)
+    for number, (source, target, whole) in enumerate(pairs):
+        for there in peers:
             pltpu.make_async_remote_copy(
-                src_ref=source if whole else source.at[there],
+                src_ref=source if whole else source.at[flat(there, sizes)],
                 dst_ref=target.at[me],
                 send_sem=send_sems.at[number],
                 recv_sem=recv_sems.at[number],
-                device_id=(there_x, there_y, there_z),
+                device_id=there,
                 device_id_type=MESH,
             ).start()
-        return carry
-
-    lax.fori_loop(1, devices, send, 0)
     for source, target, whole in pairs:
         target[me] = source[...] if whole else source[me]
     for number, (source, target, whole) in enumerate(pairs):
-        most = target.at[pl.ds(0, devices - 1)]
+        most = target.at[pl.ds(0, signals)]
         arrived = pltpu.make_async_remote_copy(
             src_ref=most, dst_ref=most, send_sem=send_sems.at[number],
             recv_sem=recv_sems.at[number], device_id=tuple(here), device_id_type=MESH,
@@ -78,96 +99,115 @@
         arrived.wait_recv()
 
 
-def fill_blocks(cell_ref, q_ref, v_ref, sendq_ref, sendv_ref):
+def fill_blocks(cell_ref, q_ref, v_ref, send_ref):
     def one(d, carry):
         first, second = cell_ref[2 * d], cell_ref[2 * d + 1]
-        sendq_ref[d, 0] = q_ref[first]
-        sendq_ref[d, 1] = q_ref[second]
+        for number, cell in enumerate((first, second)):
+            rows = q_ref[cell]
+            send_ref[d, 2 * number] = rows[0:4]
+            send_ref[d, 2 * number + 1] = rows[4:8]
         low, high = v_ref[first], v_ref[second]
-        sendv_ref[d, 0] = low[0:4]
-        sendv_ref[d, 1, 0:2] = low[4:6]
-        sendv_ref[d, 1, 2:4] = high[0:2]
-        sendv_ref[d, 2] = high[2:6]
+        send_ref[d, 4] = low[0:4]
+        send_ref[d, 5, 0:2] = low[4:6]
+        send_ref[d, 5, 2:4] = high[0:2]
+        send_ref[d, 6] = high[2:6]
         return carry
 
-    lax.fori_loop(0, sendq_ref.shape[0], one, 0)
-
-
-def velocity_rows(recvv_ref, slot):
+    lax.fori_loop(0, send_ref.shape[0], one, 0)
+
+
+def cell_rows(recv_ref, slot):
+    block, odd = slot >> 1, slot & 1
+    return [recv_ref[block, 2 * odd + half] for half in range(2)]
+
+
+def velocity_rows(recv_ref, slot):
     block, odd = slot >> 1, (slot & 1) == 1
-    first, middle, last = recvv_ref[block, 0], recvv_ref[block, 1], recvv_ref[block, 2]
+    first, middle, last = recv_ref[block, 4], recv_ref[block, 5], recv_ref[block, 6]
     even_rows = jnp.concatenate([first, middle[0:2]], axis=0)
     odd_rows = jnp.concatenate([middle[2:4], last], axis=0)
     rows = jnp.where(odd, odd_rows, even_rows)
     return rows[0:3], rows[3:6]
 
 
-def first_exchange_kernel(sizes, cell_ref, meta_ref, pos_ref, h_ref, vel_ref,
-                          recvq_ref, recvv_ref, metas_ref,
-                          q_ref, v_ref, sendq_ref, sendv_ref, send_sems, recv_sems):
-    for cell in range(pos_ref.shape[0]):
+def first_exchange_kernel(sizes, cell_ref, meta_ref, pos_ref, h_ref, vel_ref, recv_ref, metas_ref,
+                          q_ref, v_ref, send_ref, send_sems, recv_sems):
+    def fill():
+        for cell in range(pos_ref.shape[1]):
+            for half in range(2):
+                lanes = slice(half * LANES, (half + 1) * LANES)
+                for component in range(3):
+                    q_ref[cell, 4 * half + component] = pos_ref[component, cell, lanes]
+                    v_ref[cell, 3 * half + component] = vel_ref[component, cell, lanes]
+                q_ref[cell, 4 * half + 3] = h_ref[cell, lanes]
+        fill_blocks(cell_ref, q_ref, v_ref, send_ref)
+
+    pairs = ((meta_ref, metas_ref, True), (send_ref, recv_ref, False))
+    exchange(sizes, fill, pairs, send_sems, recv_sems)
+
+
+def last_exchange_kernel(sizes, cell_ref, q_ref, v_ref, recv_ref, send_ref, send_sems, recv_sems):
+    def fill():
+        fill_blocks(cell_ref, q_ref, v_ref, send_ref)
+
+    exchange(sizes, fill, ((send_ref, recv_ref, False),), send_sems, recv_sems)
+
+
+def halo(sizes, fill, pairs, send_sems, recv_sems):
+    here = [lax.axis_index(axis) for axis in AXES]
+    peers = []
+    for axis, step in neighbour_steps():
+        there = [0] * 3
+        there[AXES.index(axis)] = (-step) % sizes[AXES.index(axis)]
+        peers.append(shifted(here, there, sizes))
+    barrier, signals = greet(peers)
+    fill()
+    pl.semaphore_wait(barrier, signals)
+    copies = []
+    for which, (source, target) in enumerate(pairs):
+        for number, there in enumerate(peers):
+            copies.append(
+                pltpu.make_async_remote_copy(
+                    src_ref=source, dst_ref=target.at[number + 1],
+                    send_sem=send_sems.at[which, number], recv_sem=recv_sems.at[which, number],
+                    device_id=there, device_id_type=MESH,
+                )
+            )
+            copies[-1].start()
+    for copy in copies:
+        copy.wait()
+
+
+def cell_halo_kernel(sizes, slot_ref, count_ref, recv_ref, table_ref, counts_ref, send_sems, recv_sems):
+    def fill():
+        counts_ref[0] = count_ref[...]
+        for place in range(table_ref.shape[1]):
+            low, high = cell_rows(recv_ref, slot_ref[place])
+            table_ref[0, place, 0:4] = low
+            table_ref[0, place, 4:8] = high
+
+    pairs = ((count_ref, counts_ref), (table_ref.at[0], table_ref))
+    halo(sizes, fill, pairs, send_sems, recv_sems)
+
+
+def rho_halo_kernel(sizes, rho_ref, table_ref, send_sems, recv_sems):
+    def fill():
+        table_ref[0] = rho_ref[...]
+
+    halo(sizes, fill, ((rho_ref, table_ref),), send_sems, recv_sems)
+
+
+def unpack_kernel(slot_ref, recv_ref, pos_ref, vel_ref, rho_ref):
+    for place in range(pos_ref.shape[1]):
+        slot = slot_ref[place]
+        rows = cell_rows(recv_ref, slot)
+        velocity = velocity_rows(recv_ref, slot)
         for half in range(2):
             lanes = slice(half * LANES, (half + 1) * LANES)
-            q_ref[cell, 4 * half : 4 * half + 3] = pos_ref[cell, :, lanes]
-            q_ref[cell, 4 * half + 3 : 4 * half + 4] = h_ref[cell : cell + 1, lanes]
-            v_ref[cell, 3 * half : 3 * half + 3] = vel_ref[cell, :, lanes]
-    fill_blocks(cell_ref, q_ref, v_ref, sendq_ref, sendv_ref)
-    exchange(
-        sizes,
-        ((meta_ref, metas_ref, True), (sendq_ref, recvq_ref, False), (sendv_ref, recvv_ref, False)),
-        send_sems, recv_sems,
-    )
-
-
-def last_exchange_kernel(sizes, cell_ref, q_ref, v_ref, recvq_ref, recvv_ref,
-                         sendq_ref, sendv_ref, send_sems, recv_sems):
-    fill_blocks(cell_ref, q_ref, v_ref, sendq_ref, sendv_ref)
-    exchange(
-        sizes, ((sendq_ref, recvq_ref, False), (sendv_ref, recvv_ref, False)), send_sems, recv_sems
-    )
-
-
-def halo(sizes, own, table_ref, send_sems, recv_sems):
-    here = [lax.axis_index(axis) for axis in AXES]
-    copies = []
-    for number, (axis, step) in enumerate(neighbour_steps()):
-        there = list(here)
-        dim = AXES.index(axis)
-        there[dim] = lax.rem(here[dim] + sizes[dim] - step, sizes[dim])
-        copies.append(
-            pltpu.make_async_remote_copy(
-                src_ref=own, dst_ref=table_ref.at[number + 1], send_sem=send_sems.at[number],
-                recv_sem=recv_sems.at[number], device_id=tuple(there), device_id_type=MESH,
-            )
-        )
-        copies[-1].start()
-    return copies
-
-
-def cell_halo_kernel(sizes, slot_ref, recvq_ref, table_ref, send_sems, recv_sems):
-    for place in range(table_ref.shape[1]):
-        table_ref[0, place] = recvq_ref[slot_ref[place]]
-    for copy in halo(sizes, table_ref.at[0], table_ref, send_sems, recv_sems):
-        copy.wait()
-
-
-def rho_halo_kernel(sizes, rho_ref, table_ref, send_sems, recv_sems):
-    copies = halo(sizes, rho_ref, table_ref, send_sems, recv_sems)
-    table_ref[0] = rho_ref[...]
-    for copy in copies:
-        copy.wait()
-
-
-def unpack_kernel(slot_ref, recvq_ref, recvv_ref, pos_ref, vel_ref, rho_ref):
-    for place in range(pos_ref.shape[0]):
-        slot = slot_ref[place]
-        rows = recvq_ref[slot]
-        velocity = velocity_rows(recvv_ref, slot)
-        for half in range(2):
-            lanes = slice(half * LANES, (half + 1) * LANES)
-            pos_ref[place, :, lanes] = rows[4 * half : 4 * half + 3]
-            rho_ref[place : place + 1, lanes] = rows[4 * half + 3 : 4 * half + 4]
-            vel_ref[place, :, lanes] = velocity[half]
+            for component in range(3):
+                pos_ref[component, place, lanes] = rows[half][component]
+                vel_ref[component, place, lanes] = velocity[half][component]
+            rho_ref[place, lanes] = rows[half][3]
 
 
 def fixed_point(table_ref, fixed_ref, box):
@@ -283,7 +323,7 @@
 
 
 def accel_kernel(partners, mass, unit, shifts, box, near_ref, count_ref, slot_ref, table_ref, rho_ref,
-                 recvv_ref, q_ref, v_ref,
+                 recv_ref, q_ref, v_ref,
                  fixed_ref, inverse_ref, list_ref, inverse_list_ref, xi_ref, yi_ref, zi_ref, ci_ref, ai_ref,
                  ax_ref, ay_ref, az_ref):
     cells, particles = table_ref.shape[1], 2 * LANES
@@ -340,7 +380,7 @@
 
         lax.fori_loop(0, last, one_chunk, 0)
         scale = [(time_step * 2.0 * mass * unit) / (part * part * part * part * part) for part in h]
-        velocity = velocity_rows(recvv_ref, slot_ref[cell])
+        velocity = velocity_rows(recv_ref, slot_ref[cell])
         for component, acc_ref in enumerate(acc_refs):
             sums = row_sums(acc_ref[...])
             for half in range(2):
@@ -371,58 +411,49 @@
     smem = pl.BlockSpec(memory_space=pltpu.SMEM)
     vmem = pl.BlockSpec(memory_space=pltpu.VMEM)
     f32 = lambda *shape: jax.ShapeDtypeStruct(shape, jnp.float32)
-    effects = pltpu.CompilerParams(has_side_effects=True)
-    sems = lambda count: [pltpu.SemaphoreType.DMA((count,))] * 2
-    blocks_q, blocks_v = (devices, 2, 8, LANES), (devices, 3, 4, LANES)
-    sends = [pltpu.VMEM(blocks_q, jnp.float32), pltpu.VMEM(blocks_v, jnp.float32)]
+    effects = lambda number: pltpu.CompilerParams(has_side_effects=True, collective_id=number)
+    sems = lambda *count: [pltpu.SemaphoreType.DMA(count)] * 2
+    blocks = (devices, 7, 4, LANES)
     cells8 = pltpu.VMEM((cell_count, 8, LANES), jnp.float32)
 
-    key_before, cell_before = slots_of(plan_before, cell_count, devices)
-    key_after, cell_after = slots_of(plan_after, cell_count, devices)
-    meta = jnp.concatenate([key_before, key_after, counts, jnp.zeros_like(counts)])[None, :]
-    recv_q, recv_v, metas = pl.pallas_call(
+    keys, cells = slots_of(jnp.stack([plan_before, plan_after]), cell_count, devices)
+    meta = jnp.concatenate([keys.reshape(-1), counts, jnp.zeros_like(counts)])[None, :]
+    recv, metas = pl.pallas_call(
         functools.partial(first_exchange_kernel, sizes),
-        out_shape=[f32(*blocks_q), f32(*blocks_v), jax.ShapeDtypeStruct((devices, 1, LANES), jnp.int32)],
+        out_shape=[f32(*blocks), jax.ShapeDtypeStruct((devices, 1, LANES), jnp.int32)],
         in_specs=[smem, vmem, vmem, vmem, vmem],
-        out_specs=[vmem] * 3,
-        scratch_shapes=[cells8, cells8] + sends + sems(3),
-        compiler_params=effects,
+        out_specs=[vmem] * 2,
+        scratch_shapes=[cells8, cells8, pltpu.VMEM(blocks, jnp.float32)] + sems(2),
+        compiler_params=effects(0),
         name="first_exchange",
-    )(cell_before, meta, positions, smoothing, velocity)
+    )(cells[0], meta, jnp.transpose(positions, (1, 0, 2)), smoothing, jnp.transpose(velocity, (1, 0, 2)))
 
     here = [lax.axis_index(axis) for axis in AXES]
-    blocks = [tuple(here)]
-    for axis, step in neighbour_steps():
-        there = list(here)
-        dim = AXES.index(axis)
-        there[dim] = (here[dim] + step) % sizes[dim]
-        blocks.append(tuple(there))
-    first_place = jnp.stack([((x * sizes[1] + y) * sizes[2] + z) * cell_count for x, y, z in blocks])
-    local = jnp.arange(cell_count, dtype=jnp.int32)
-    place = (first_place[:, None] + local[None, :]).reshape(-1)
-    keys, keys_after = metas[:, 0, 0:cell_count], metas[:, 0, cell_count : 2 * cell_count]
-    all_counts = metas[:, 0, 2 * cell_count : 3 * cell_count]
-    source = 2 * jnp.arange(devices, dtype=jnp.int32)[None, :, None]
-
-    def pick(keys, places, values):
-        hit = (keys >> 1)[None] == places[:, None, None]
-        return jnp.sum(jnp.where(hit, values, 0), axis=(1, 2))
-
-    own_place = place[:cell_count]
-    table_count = pick(keys, place, all_counts[None])
-    slot_before = pick(keys, own_place, (keys & 1)[None] + source)
-    slot_after = pick(keys_after, own_place, (keys_after & 1)[None] + source)
+    place = flat(here, sizes) * cell_count + jnp.arange(cell_count, dtype=jnp.int32)
+    metas = metas[:, 0, :]
+    keys_before, keys_after = metas[:, 0:cell_count], metas[:, cell_count : 2 * cell_count]
+    all_counts = metas[:, 2 * cell_count : 3 * cell_count]
+    source = 2 * jnp.arange(devices, dtype=jnp.int32)[:, None]
+
+    def pick(keys, values):
+        hit = (keys >> 1)[None] == place[:, None, None]
+        return jnp.sum(jnp.where(hit, values[None], 0), axis=(1, 2))
+
+    slot_count = pick(keys_before, (keys_before & 1) + source + all_counts * (2 * devices))
+    slot_before, own_count = slot_count % (2 * devices), slot_count // (2 * devices)
+    slot_after = pick(keys_after, (keys_after & 1) + source)
     near = near_table(neighbours, cell_count)
 
-    table = pl.pallas_call(
+    table, table_count = pl.pallas_call(
         functools.partial(cell_halo_kernel, sizes),
-        out_shape=f32(7, cell_count, 8, LANES),
-        in_specs=[smem, vmem],
-        out_specs=vmem,
-        scratch_shapes=sems(6),
-        compiler_params=effects,
+        out_shape=[f32(7, cell_count, 8, LANES), jax.ShapeDtypeStruct((7, 1, LANES), jnp.int32)],
+        in_specs=[smem, vmem, vmem],
+        out_specs=[vmem, vmem],
+        scratch_shapes=sems(2, 6),
+        compiler_params=effects(1),
         name="cell_halo",
-    )(slot_before, recv_q.reshape(2 * devices, 8, LANES))
+    )(slot_before, jnp.pad(own_count, (0, LANES - cell_count))[None, :], recv)
+    table_count = table_count[:, 0, :cell_count].reshape(-1)
 
     chunks = partners * particles // LANES + 1
     square = (particles, LANES)
@@ -443,8 +474,8 @@
         out_shape=f32(7, cell_count, 2, LANES),
         in_specs=[vmem],
         out_specs=vmem,
-        scratch_shapes=sems(6),
-        compiler_params=effects,
+        scratch_shapes=sems(1, 6),
+        compiler_params=effects(2),
         name="rho_halo",
     )(rho)
 
@@ -462,24 +493,25 @@
         + columns
         + [pltpu.VMEM(square, jnp.float32)] * 5,
         name="accel",
-    )(near, table_count, slot_before, table, table_rho, recv_v)
-
-    last_q, last_v = pl.pallas_call(
+    )(near, table_count, slot_before, table, table_rho, recv)
+
+    last = pl.pallas_call(
         functools.partial(last_exchange_kernel, sizes),
-        out_shape=[f32(*blocks_q), f32(*blocks_v)],
+        out_shape=f32(*blocks),
         in_specs=[smem, vmem, vmem],
-        out_specs=[vmem] * 2,
-        scratch_shapes=sends + sems(2),
-        compiler_params=effects,
+        out_specs=vmem,
+        scratch_shapes=[pltpu.VMEM(blocks, jnp.float32)] + sems(1),
+        compiler_params=effects(3),
         name="last_exchange",
-    )(cell_after, out_q, out_v)
-    return pl.pallas_call(
+    )(cells[1], out_q, out_v)
+    new_pos, new_vel, new_rho = pl.pallas_call(
         unpack_kernel,
-        out_shape=[f32(*positions.shape), f32(*velocity.shape), f32(*smoothing.shape)],
-        in_specs=[smem, vmem, vmem],
+        out_shape=[f32(3, cell_count, particles)] * 2 + [f32(cell_count, particles)],
+        in_specs=[smem, vmem],
         out_specs=[vmem] * 3,
         name="unpack",
-    )(slot_after, last_q.reshape(2 * devices, 8, LANES), last_v)
+    )(slot_after, last)
+    return jnp.transpose(new_pos, (1, 0, 2)), jnp.transpose(new_vel, (1, 0, 2)), new_rho
 
 
 def solution(mesh):

time: 255 us -> 207 us (0.81)
  Pallas kernels: 230 us -> 193 us
  other arithmetic: 15.8 us -> 7.15 us
  local copies, waits for them, and re-layouts: 7.59 us -> 3.57 us
    pallas_call x1, Pallas kernels: 48.9 us -> 35.1 us  [shards(): pl.pallas_call(functools.partial(last_exchange_kernel, sizes), out_shape=...]
    pallas_call x1, Pallas kernels: 49.4 us -> 35.7 us  [shards(): pl.pallas_call(functools.partial(first_exchange_kernel, sizes), out_shape...]
    reduce_sum x6 -> x3, other arithmetic: 8.56 us -> 2.11 us  [the longest x1 1.84 us: pick(): return jnp.sum(jnp.where(hit, values[None], 0), axis=(1, 2))]
    pallas_call x1, Pallas kernels: 15.6 us -> 10.4 us  [shards(): pl.pallas_call(functools.partial(rho_halo_kernel, sizes), out_shape=f32(7...]
    unnamed x2 -> x0, local copies, waits for them, and re-layouts: 3.22 us -> none
    pallas_call x2 -> x0, local copies, waits for them, and re-layouts: 3.13 us -> none  [shards(): pl.pallas_call(unpack_kernel, out_shape=[f32(*positions.shape), f32(*velo...]
    pallas_call x2, Pallas kernels: 14.5 us -> 11.6 us  [the longest x1 9.22 us: shards(): pl.pallas_call(functools.partial(cell_halo_kernel, sizes), out_shape=[f32...]
where the time goes in v3:
time: 207 us; the launch traced here: 205 us
  Pallas kernels  193 us (93%)
  other arithmetic  7.15 us (3%)
  local copies, waits for them, and re-layouts  3.57 us (2%)
    pallas_call x1, Pallas kernels, shards(): pl.pallas_call(functools.partial(accel_kernel, partners, mass, unit, shif...  58.9 us
    pallas_call x1, Pallas kernels, shards(): pl.pallas_call(functools.partial(density_kernel, partners, mass, unit, sh...  41.2 us
    pallas_call x1, Pallas kernels, shards(): pl.pallas_call(functools.partial(first_exchange_kernel, sizes), out_shape...  35.7 us
    pallas_call x1, Pallas kernels, shards(): pl.pallas_call(functools.partial(last_exchange_kernel, sizes), out_shape=...  35.1 us
    pallas_call x1, Pallas kernels, shards(): pl.pallas_call(functools.partial(rho_halo_kernel, sizes), out_shape=f32(7...  10.4 us
    pallas_call x1, Pallas kernels, shards(): pl.pallas_call(functools.partial(cell_halo_kernel, sizes), out_shape=[f32...  9.22 us

profile of v3, /device:TPU:1, one launch (start us, length us, event | category | flops | bytes accessed | tf_op | source)
XLA Modules:
  0.0 204.5 jit_solution(8710704577633682614)
XLA Ops:
  0.8 0.7 and_select_fusion.2
  1.5 0.7 fusion.1
  2.2 0.2 convert_reduce_fusion
  2.4 0.7 multiply_add_fusion
  3.1 0.1 add.151
  3.2 1.3 add_bitcast_fusion.meta_ref
  4.5 0.1 select_reduce_fusion.2
  4.6 0.6 fusion.3
  5.1 0.1 copy.20
  5.2 0.7 reshape.214.near_ref
  5.9 35.7 %first_exchange.1 = (f32[128,7,4,128]{3,2,1,0:T(4,128)}, s32[128,1,128]{2,1,0:T(1,128)}) custom-call(s32[256]{0:T(256)} %bitcast.17, s32[1,128]{1,0:T(1,128)} %add_bitcast_fusion.meta_ref, f32[3,32,256]{2,1,0:T(8,128)} %bitcast.14, f32[32,256]{1,0:T(8,128)} %h_ref.1, f32[3,32,256]{2,1,0:T(8,128)} %bitcast.15), custom_call_target="tpu_custom_call" | custom-call | tf_op jit(solution)/shard_map/first_exchange/pallas_call | solution.py:421
  41.6 1.1 and_add_fusion
  42.9 0.1 copy.17
  43.0 1.8 select_reduce_fusion
  44.8 0.5 and_select_fusion
  45.4 0.5 pad_bitcast_fusion.count_ref
  45.9 9.2 %cell_halo.1 = (f32[7,32,8,128]{3,2,1,0:T(8,128)}, s32[7,1,128]{2,1,0:T(1,128)}) custom-call(s32[32]{0:T(128)} %get-tuple-element.32.slot_ref, s32[1,128]{1,0:T(1,128)} %pad_bitcast_fusion.count_ref, f32[128,7,4,128]{3,2,1,0:T(4,128)} %get-tuple-element.13.recv_ref), custom_call_target="tpu_custom_call" | custom-call | tf_op jit(solution)/shard_map/cell_halo/pallas_call | solution.py:447
  55.1 0.7 slice_reduce_fusion
  55.8 0.7 reshape_squeeze.3.count_ref
  56.5 41.2 %density.1.rho_ref = f32[32,2,128]{2,1,0:T(2,128)} custom-call(s32[288]{0:T(512)} %reshape.214.near_ref, s32[224]{0:T(256)} %reshape_squeeze.3.count_ref, f32[7,32,8,128]{3,2,1,0:T(8,128)} %get-tuple-element.15.table_ref), custom_call_target="tpu_custom_call" | custom-call | tf_op jit(solution)/shard_map/density/pallas_call | solution.py:462
  97.7 10.4 %rho_halo.1.rho_ref = f32[7,32,2,128]{3,2,1,0:T(2,128)} custom-call(f32[32,2,128]{2,1,0:T(2,128)} %density.1.rho_ref), custom_call_target="tpu_custom_call" | custom-call | tf_op jit(solution)/shard_map/rho_halo/pallas_call | solution.py:472
  108.1 58.9 %accel.1 = (f32[32,8,128]{2,1,0:T(8,128)}, f32[32,8,128]{2,1,0:T(8,128)}) custom-call(s32[288]{0:T(512)} %reshape.214.near_ref, s32[224]{0:T(256)} %reshape_squeeze.3.count_ref, s32[32]{0:T(128)} %get-tuple-element.32.slot_ref, f32[7,32,8,128]{3,2,1,0:T(8,128)} %get-tuple-element.15.table_ref, f32[7,32,2,128]{3,2,1,0:T(2,128)} %rho_halo.1.rho_ref, ...), custom_call_target="tpu_custom_call" | custom-call | tf_op jit(solution)/shard_map/accel/pallas_call | solution.py:482
  167.0 35.1 %last_exchange.1.recv_ref = f32[128,7,4,128]{3,2,1,0:T(4,128)} custom-call(s32[256]{0:T(256)} %bitcast.16, f32[32,8,128]{2,1,0:T(8,128)} %get-tuple-element.16.q_ref, f32[32,8,128]{2,1,0:T(8,128)} %get-tuple-element.17.v_ref), custom_call_target="tpu_custom_call" | custom-call | tf_op jit(solution)/shard_map/last_exchange/pallas_call | solution.py:498
  202.1 2.4 %unpack.1 = (f32[3,32,256]{2,1,0:T(8,128)}, f32[3,32,256]{2,1,0:T(8,128)}, f32[32,256]{1,0:T(8,128)}) custom-call(s32[32]{0:T(128)} %get-tuple-element.22.slot_ref, f32[128,7,4,128]{3,2,1,0:T(4,128)} %last_exchange.1.recv_ref), custom_call_target="tpu_custom_call" | custom-call | tf_op jit(solution)/shard_map/unpack/pallas_call | solution.py:507
  (9 shorter events, 0.2 us)

commit v4 on v3

--- a/solution.py
+++ b/solution.py
@@ -279,8 +279,232 @@
     return parts
 
 
+def by_row(values):
+    row = lax.broadcasted_iota(jnp.int32, (8, LANES), 0) & 3
+    out = jnp.full((8, LANES), values[3], jnp.float32)
+    for number in range(3):
+        out = jnp.where(row == number, jnp.float32(values[number]), out)
+    return out
+
+
+def bounds(table_ref, low_ref, high_ref):
+    blocks, cells = table_ref.shape[0], table_ref.shape[1]
+
+    def one(cell, carry):
+        for block in range(blocks):
+            rows = table_ref[block, cell]
+            low = jnp.broadcast_to(jnp.min(rows, axis=1, keepdims=True), (8, LANES))
+            high = jnp.broadcast_to(jnp.max(rows, axis=1, keepdims=True), (8, LANES))
+            low_ref[block * cells + cell] = jnp.minimum(low, pltpu.roll(low, 4, 0))
+            high_ref[block * cells + cell] = jnp.maximum(high, pltpu.roll(high, 4, 0))
+        return carry
+
+    lax.fori_loop(0, cells, one, 0)
+
+
+def middle(low, high):
+    return jnp.floor(low + high + 0.5) * 0.5
+
+
+def image(low_a, high_a, low_b, high_b, lengths):
+    return jnp.floor((low_a - high_b) / lengths + 0.5) * lengths
+
+
+def sum_of_xyz(rows):
+    return pltpu.roll(rows, 1, 0) + pltpu.roll(rows, 2, 0) + pltpu.roll(rows, 3, 0)
+
+
+def one_image(cells, partners, box, near_ref, low_ref, high_ref):
+    lengths = by_row(box + (1.0,))
+    half = lengths * (0.5 * (1.0 - 2.0**-16))
+    coordinate = (lax.broadcasted_iota(jnp.int32, (8, LANES), 0) & 3) < 3
+    limit = 256.0 / math.log2(math.e)
+
+    def one(cell, good):
+        low_a, high_a = low_ref[cell], high_ref[cell]
+        origin = middle(low_a, high_a)
+        for partner in range(partners):
+            b = near_ref[cell * partners + partner]
+            low_b, high_b = low_ref[b], high_ref[b]
+            shift = image(low_a, high_a, low_b, high_b, lengths)
+            fits = (high_a - low_b - shift < half) & (low_a - high_b - shift > -half)
+            moved = shift - origin
+            reach = jnp.maximum(jnp.abs(low_b + moved), jnp.abs(high_b + moved))
+            small = sum_of_xyz(reach * reach) <= limit * low_a * low_a
+            fine = jnp.where(coordinate, jnp.where(fits, 1.0, 0.0), jnp.where(small, 1.0, 0.0))
+            good = jnp.minimum(good, fine)
+        return good
+
+    good = lax.fori_loop(0, cells, one, jnp.ones((8, LANES), jnp.float32))
+    return jnp.min(good) > 0.5
+
+
+def three_parts(value):
+    first = value.astype(jnp.bfloat16).astype(jnp.float32)
+    value = value - first
+    second = value.astype(jnp.bfloat16).astype(jnp.float32)
+    return first, second, value - second
+
+
+def joined(upper, lower, half):
+    top = lax.broadcasted_iota(jnp.int32, (8, LANES), 0) < 4
+    if half == 0:
+        return jnp.where(top, upper, pltpu.roll(lower, 4, 0))
+    return jnp.where(top, pltpu.roll(upper, 4, 0), lower)
+
+
+def own_factors(rows, origin, own_ref):
+    row = lax.broadcasted_iota(jnp.int32, (8, LANES), 0)
+    centred = rows - origin
+    c = -math.log2(math.e) / (rows * rows)
+    c = jnp.where(row < 4, jnp.broadcast_to(c[3:4], (8, LANES)), jnp.broadcast_to(c[7:8], (8, LANES)))
+    p1, p2, p3 = three_parts(jnp.where((row & 3) == 3, c, -2.0 * c * centred))
+    squares = three_parts(c * sum_of_xyz(centred * centred))
+    for half in range(2):
+        last = jnp.where(row == 3, 1.0, 0.0)
+        for number, part in enumerate(squares):
+            moved = pltpu.roll(part, (number + 5 - 4 * half) % 8, 0)
+            last = jnp.where(row == number, moved, last)
+        groups = [joined(p1, p1, half), joined(p1, p2, half), joined(p2, p3, half), last]
+        block = jnp.concatenate(groups, axis=0).T
+        own_ref[half * LANES : (half + 1) * LANES, :] = block.astype(jnp.bfloat16)
+    return centred
+
+
+def near_factors(moved, live, near_ref, partner):
+    row = lax.broadcasted_iota(jnp.int32, (8, LANES), 0)
+    lane = lax.broadcasted_iota(jnp.int32, (8, LANES), 1)
+    q1, q2, q3 = three_parts(jnp.where((row & 3) == 3, sum_of_xyz(moved * moved), moved))
+    for half in range(2):
+        alive = lane + half * LANES < live
+        last = jnp.where(row < 3, 1.0, jnp.where((row > 3) | alive, 0.0, -1e30))
+        groups = [joined(q1, q2, half), joined(q3, q1, half), joined(q2, q1, half), last]
+        block = jnp.concatenate(groups, axis=0)
+        near_ref[partner, :, half * LANES : (half + 1) * LANES] = block.astype(jnp.bfloat16)
+
+
+def exponents(own_ref, near_ref, partner, rows):
+    return jnp.dot(own_ref[rows, :], near_ref[partner], preferred_element_type=jnp.float32)
+
+
+def lane_sums(acc):
+    ones = jnp.ones((8, LANES), jnp.bfloat16)
+    total = jnp.zeros((8, 2 * LANES), jnp.float32)
+    for part in reversed(three_parts(acc)):
+        total = total + lax.dot_general(
+            ones, part.astype(jnp.bfloat16), (((1,), (1,)), ((), ())),
+            preferred_element_type=jnp.float32,
+        )
+    return [total[0:1, 0:LANES], total[0:1, LANES : 2 * LANES]]
+
+
+def fast_density(cells, partners, mass, box, near_ref, count_ref, table_ref, low_ref, high_ref, rho_ref,
+                 own_ref, factor_ref, acc_ref):
+    lengths = by_row(box + (1.0,))
+    step = 64
+
+    def one_cell(cell, carry):
+        low_a, high_a = low_ref[cell], high_ref[cell]
+        origin = middle(low_a, high_a)
+        own_factors(table_ref[0, cell], origin, own_ref)
+        for partner in range(partners):
+            b = near_ref[cell * partners + partner]
+            shift = image(low_a, high_a, low_ref[b], high_ref[b], lengths)
+            moved = table_ref[b >> 5, b & 31] + (shift - origin)
+            near_factors(moved, count_ref[b], factor_ref, partner)
+        for block in range(2 * LANES // step):
+            rows = slice(block * step, (block + 1) * step)
+            acc = None
+            for partner in range(partners):
+                w = jnp.exp2(exponents(own_ref, factor_ref, partner, rows))
+                both = w[:, 0:LANES] + w[:, LANES : 2 * LANES]
+                acc = both if acc is None else acc + both
+            acc_ref[rows, :] = acc
+        h = halves_of(table_ref.at[0], cell, 3)
+        for half, (part, total) in enumerate(zip(h, lane_sums(acc_ref[...]))):
+            rho_ref[cell, half : half + 1] = mass * (1.0 + total) / (part * part * part)
+        return carry
+
+    lax.fori_loop(0, cells, one_cell, 0)
+
+
+def fast_accel(cells, partners, mass, box, near_ref, count_ref, slot_ref, table_ref, low_ref, high_ref,
+               inverse_ref, rho_ref, recv_ref, q_ref, v_ref,
+               own_ref, factor_ref, moved_ref, ai_ref, acc_refs):
+    lengths = by_row(box + (1.0,))
+    step = 32
+
+    def one_cell(cell, carry):
+        low_a, high_a = low_ref[cell], high_ref[cell]
+        origin = middle(low_a, high_a)
+        centred = own_factors(table_ref[0, cell], origin, own_ref)
+        store_column(ai_ref, halves_of(inverse_ref, cell, 0))
+        for partner in range(partners):
+            b = near_ref[cell * partners + partner]
+            shift = image(low_a, high_a, low_ref[b], high_ref[b], lengths)
+            moved = table_ref[b >> 5, b & 31] + (shift - origin)
+            near_factors(moved, count_ref[b], factor_ref, partner)
+            moved_ref[partner] = moved
+            for half in range(2):
+                moved_ref[partner, 4 * half + 3 : 4 * half + 4] = inverse_ref[b, half : half + 1]
+        for block in range(2 * LANES // step):
+            rows = slice(block * step, (block + 1) * step)
+            own_inverse = ai_ref[rows, :]
+            accs = [None] * 4
+            for partner in range(partners):
+                w = jnp.exp2(exponents(own_ref, factor_ref, partner, rows))
+                for half in range(2):
+                    near = [
+                        jnp.broadcast_to(
+                            moved_ref[partner, 4 * half + row : 4 * half + row + 1, :], (step, LANES)
+                        )
+                        for row in range(4)
+                    ]
+                    pair = w[:, half * LANES : (half + 1) * LANES] * (own_inverse + near[3])
+                    terms = [pair * near[0], pair * near[1], pair * near[2], pair]
+                    accs = [t if a is None else a + t for a, t in zip(accs, terms)]
+            for acc_ref, acc in zip(acc_refs, accs):
+                acc_ref[rows, :] = acc
+        h = halves_of(table_ref.at[0], cell, 3)
+        scale = [(time_step * 2.0 * mass) / (part * part * part * part * part) for part in h]
+        velocity = velocity_rows(recv_ref, slot_ref[cell])
+        whole = lane_sums(acc_refs[3][...])
+        for component in range(3):
+            sums = lane_sums(acc_refs[component][...])
+            for half in range(2):
+                row = slice(4 * half + component, 4 * half + component + 1)
+                force = centred[row] * whole[half] - sums[half]
+                kicked = velocity[half][component : component + 1] + force * scale[half]
+                v_ref[cell, 3 * half + component : 3 * half + component + 1] = kicked
+                q_ref[cell, row] = table_ref[0, cell, row] + time_step * kicked
+        for half in range(2):
+            row = slice(4 * half + 3, 4 * half + 4)
+            q_ref[cell, row] = rho_ref[0, cell, half : half + 1]
+        return carry
+
+    lax.fori_loop(0, cells, one_cell, 0)
+
+
 def density_kernel(partners, mass, unit, shifts, box, near_ref, count_ref, table_ref, rho_ref,
+                   low_ref, high_ref, own_ref, factor_ref,
                    fixed_ref, list_ref, xi_ref, yi_ref, zi_ref, ci_ref, acc_ref):
+    cells = table_ref.shape[1]
+    bounds(table_ref, low_ref, high_ref)
+    fits = one_image(cells, partners, box, near_ref, low_ref, high_ref)
+
+    @pl.when(fits)
+    def _():
+        fast_density(cells, partners, mass, box, near_ref, count_ref, table_ref, low_ref, high_ref,
+                     rho_ref, own_ref, factor_ref, acc_ref)
+
+    @pl.when(jnp.logical_not(fits))
+    def _():
+        any_density(partners, mass, unit, shifts, box, near_ref, count_ref, table_ref, rho_ref,
+                    fixed_ref, list_ref, xi_ref, yi_ref, zi_ref, ci_ref, acc_ref)
+
+
+def any_density(partners, mass, unit, shifts, box, near_ref, count_ref, table_ref, rho_ref,
+                fixed_ref, list_ref, xi_ref, yi_ref, zi_ref, ci_ref, acc_ref):
     cells, particles = table_ref.shape[1], 2 * LANES
     blocks = particles // 8
     i_refs = (xi_ref, yi_ref, zi_ref)
@@ -323,6 +547,35 @@
 
 
 def accel_kernel(partners, mass, unit, shifts, box, near_ref, count_ref, slot_ref, table_ref, rho_ref,
+                 recv_ref, q_ref, v_ref,
+                 low_ref, high_ref, own_ref, factor_ref, moved_ref, sum_ref,
+                 fixed_ref, inverse_ref, list_ref, inverse_list_ref, xi_ref, yi_ref, zi_ref, ci_ref, ai_ref,
+                 ax_ref, ay_ref, az_ref):
+    cells = table_ref.shape[1]
+    bounds(table_ref, low_ref, high_ref)
+    fits = one_image(cells, partners, box, near_ref, low_ref, high_ref)
+
+    def invert(cell, carry):
+        for block in range(rho_ref.shape[0]):
+            inverse_ref[block * cells + cell] = 1.0 / rho_ref[block, cell]
+        return carry
+
+    lax.fori_loop(0, cells, invert, 0)
+
+    @pl.when(fits)
+    def _():
+        fast_accel(cells, partners, mass, box, near_ref, count_ref, slot_ref, table_ref, low_ref, high_ref,
+                   inverse_ref, rho_ref, recv_ref, q_ref, v_ref,
+                   own_ref, factor_ref, moved_ref, ai_ref, (ax_ref, ay_ref, az_ref, sum_ref))
+
+    @pl.when(jnp.logical_not(fits))
+    def _():
+        any_accel(partners, mass, unit, shifts, box, near_ref, count_ref, slot_ref, table_ref, rho_ref,
+                  recv_ref, q_ref, v_ref, fixed_ref, inverse_ref, list_ref, inverse_list_ref,
+                  xi_ref, yi_ref, zi_ref, ci_ref, ai_ref, ax_ref, ay_ref, az_ref)
+
+
+def any_accel(partners, mass, unit, shifts, box, near_ref, count_ref, slot_ref, table_ref, rho_ref,
                  recv_ref, q_ref, v_ref,
                  fixed_ref, inverse_ref, list_ref, inverse_list_ref, xi_ref, yi_ref, zi_ref, ci_ref, ai_ref,
                  ax_ref, ay_ref, az_ref):
@@ -333,13 +586,6 @@
     lane = lax.broadcasted_iota(jnp.int32, (8, LANES), 1)
     factor = -math.log2(math.e) * unit * unit
     fixed_point(table_ref, fixed_ref, box)
-
-    def invert(cell, carry):
-        for block in range(rho_ref.shape[0]):
-            inverse_ref[block * cells + cell] = 1.0 / rho_ref[block, cell]
-        return carry
-
-    lax.fori_loop(0, cells, invert, 0)
 
     def one_cell(cell, carry):
         total = gather_live(
@@ -458,13 +704,17 @@
     chunks = partners * particles // LANES + 1
     square = (particles, LANES)
     columns = [pltpu.VMEM(square, jnp.int32)] * 3
+    extent = [pltpu.VMEM((7 * cell_count, 8, LANES), jnp.float32)] * 2 + [
+        pltpu.VMEM((particles, 32), jnp.bfloat16),
+        pltpu.VMEM((partners, 32, particles), jnp.bfloat16),
+    ]
     fixed = pltpu.VMEM((7 * cell_count, 8, LANES), jnp.int32)
     rho = pl.pallas_call(
         functools.partial(density_kernel, partners, mass, unit, shifts, box),
         out_shape=f32(cell_count, 2, LANES),
         in_specs=[smem, smem, vmem],
         out_specs=vmem,
-        scratch_shapes=[fixed, pltpu.VMEM((chunks, 4, LANES), jnp.int32)] + columns
+        scratch_shapes=extent + [fixed, pltpu.VMEM((chunks, 4, LANES), jnp.int32)] + columns
         + [pltpu.VMEM(square, jnp.float32)] * 2,
         name="density",
     )(near, table_count, table)
@@ -484,7 +734,10 @@
         out_shape=[f32(cell_count, 8, LANES)] * 2,
         in_specs=[smem, smem, smem, vmem, vmem, vmem],
         out_specs=[vmem, vmem],
-        scratch_shapes=[
+        scratch_shapes=extent
+        + [
+            pltpu.VMEM((partners, 8, LANES), jnp.float32),
+            pltpu.VMEM(square, jnp.float32),
             fixed,
             pltpu.VMEM((7 * cell_count, 2, LANES), jnp.float32),
             pltpu.VMEM((chunks, 4, LANES), jnp.int32),

time: 207 us -> 181 us (0.87)
  Pallas kernels: 193 us -> 169 us
    pallas_call x1, Pallas kernels: 41.2 us -> 29.6 us  [shards(): pl.pallas_call(functools.partial(density_kernel, partners, mass, unit, sh...]
    pallas_call x1, Pallas kernels: 35.1 us -> 30.1 us  [shards(): pl.pallas_call(functools.partial(last_exchange_kernel, sizes), out_shape=...]
    pallas_call x1, Pallas kernels: 58.9 us -> 54.7 us  [shards(): pl.pallas_call(functools.partial(accel_kernel, partners, mass, unit, shif...]
    pallas_call x1, Pallas kernels: 10.4 us -> 6.87 us  [shards(): pl.pallas_call(functools.partial(rho_halo_kernel, sizes), out_shape=f32(7...]
where the time goes in v4:
time: 181 us; the launch traced here: 180 us
  Pallas kernels  169 us (93%)
  other arithmetic  7.15 us (4%)
  local copies, waits for them, and re-layouts  3.57 us (2%)
    pallas_call x1, Pallas kernels, shards(): pl.pallas_call(functools.partial(accel_kernel, partners, mass, unit, shif...  54.7 us
    pallas_call x1, Pallas kernels, shards(): pl.pallas_call(functools.partial(first_exchange_kernel, sizes), out_shape...  35.7 us
    pallas_call x1, Pallas kernels, shards(): pl.pallas_call(functools.partial(last_exchange_kernel, sizes), out_shape=...  30.1 us
    pallas_call x1, Pallas kernels, shards(): pl.pallas_call(functools.partial(density_kernel, partners, mass, unit, sh...  29.6 us
    pallas_call x1, Pallas kernels, shards(): pl.pallas_call(functools.partial(cell_halo_kernel, sizes), out_shape=[f32...  9.22 us
    pallas_call x1, Pallas kernels, shards(): pl.pallas_call(functools.partial(rho_halo_kernel, sizes), out_shape=f32(7...  6.87 us

profile of v4, /device:TPU:1, one launch (start us, length us, event | category | flops | bytes accessed | tf_op | source)
XLA Modules:
  0.0 180.1 jit_solution(15489163482537030625)
XLA Ops:
  0.8 0.7 and_select_fusion.2
  1.5 0.7 fusion.1
  2.2 0.2 convert_reduce_fusion
  2.4 0.7 multiply_add_fusion
  3.1 0.1 add.151
  3.2 1.3 add_bitcast_fusion.meta_ref
  4.5 0.1 select_reduce_fusion.2
  4.6 0.6 fusion.3
  5.1 0.1 copy.20
  5.2 0.7 reshape.214.near_ref
  5.9 35.7 %first_exchange.1 = (f32[128,7,4,128]{3,2,1,0:T(4,128)}, s32[128,1,128]{2,1,0:T(1,128)}) custom-call(s32[256]{0:T(256)} %bitcast.17, s32[1,128]{1,0:T(1,128)} %add_bitcast_fusion.meta_ref, f32[3,32,256]{2,1,0:T(8,128)} %bitcast.14, f32[32,256]{1,0:T(8,128)} %h_ref.1, f32[3,32,256]{2,1,0:T(8,128)} %bitcast.15), custom_call_target="tpu_custom_call" | custom-call | tf_op jit(solution)/shard_map/first_exchange/pallas_call | solution.py:667
  41.6 1.1 and_add_fusion
  42.9 0.1 copy.17
  43.0 1.8 %select_reduce_fusion = (s32[32]{0:T(128)S(1)}, s32[32]{0:T(128)}) fusion(s32[128,32]{0,1:T(8,128)S(1)} %copy.24, s32[128,32]{0,1:T(8,128)S(1)} %copy.22, s32[32]{0:T(128)S(1)} %iota_add_fusion, s32[128,32]{0,1:T(8,128)S(1)} %copy.19, s32[128,32]{0,1:T(8,128)S(1)} %copy.17), kind=kLoop, calls=%fused_computation | loop fusion | flops 786368 | bytes 65920 | tf_op jit(solution)/shard_map/reduce_sum | solution.py:686
  44.8 0.5 and_select_fusion
  45.4 0.5 pad_bitcast_fusion.count_ref
  45.9 9.2 %cell_halo.1 = (f32[7,32,8,128]{3,2,1,0:T(8,128)}, s32[7,1,128]{2,1,0:T(1,128)}) custom-call(s32[32]{0:T(128)} %get-tuple-element.32.slot_ref, s32[1,128]{1,0:T(1,128)} %pad_bitcast_fusion.count_ref, f32[128,7,4,128]{3,2,1,0:T(4,128)} %get-tuple-element.13.recv_ref), custom_call_target="tpu_custom_call" | custom-call | tf_op jit(solution)/shard_map/cell_halo/pallas_call | solution.py:693
  55.1 0.7 slice_reduce_fusion
  55.8 0.7 reshape_squeeze.3.count_ref
  56.5 29.6 %density.1.rho_ref = f32[32,2,128]{2,1,0:T(2,128)} custom-call(s32[288]{0:T(512)} %reshape.214.near_ref, s32[224]{0:T(256)} %reshape_squeeze.3.count_ref, f32[7,32,8,128]{3,2,1,0:T(8,128)} %get-tuple-element.15.table_ref), custom_call_target="tpu_custom_call" | custom-call | tf_op jit(solution)/shard_map/density/pallas_call | solution.py:712
  86.0 6.9 %rho_halo.1.rho_ref = f32[7,32,2,128]{3,2,1,0:T(2,128)} custom-call(f32[32,2,128]{2,1,0:T(2,128)} %density.1.rho_ref), custom_call_target="tpu_custom_call" | custom-call | tf_op jit(solution)/shard_map/rho_halo/pallas_call | solution.py:722
  92.9 54.7 %accel.1 = (f32[32,8,128]{2,1,0:T(8,128)}, f32[32,8,128]{2,1,0:T(8,128)}) custom-call(s32[288]{0:T(512)} %reshape.214.near_ref, s32[224]{0:T(256)} %reshape_squeeze.3.count_ref, s32[32]{0:T(128)} %get-tuple-element.32.slot_ref, f32[7,32,8,128]{3,2,1,0:T(8,128)} %get-tuple-element.15.table_ref, f32[7,32,2,128]{3,2,1,0:T(2,128)} %rho_halo.1.rho_ref, ...), custom_call_target="tpu_custom_call" | custom-call | tf_op jit(solution)/shard_map/accel/pallas_call | solution.py:732
  147.6 30.1 %last_exchange.1.recv_ref = f32[128,7,4,128]{3,2,1,0:T(4,128)} custom-call(s32[256]{0:T(256)} %bitcast.16, f32[32,8,128]{2,1,0:T(8,128)} %get-tuple-element.16.q_ref, f32[32,8,128]{2,1,0:T(8,128)} %get-tuple-element.17.v_ref), custom_call_target="tpu_custom_call" | custom-call | tf_op jit(solution)/shard_map/last_exchange/pallas_call | solution.py:751
  177.7 2.4 %unpack.1 = (f32[3,32,256]{2,1,0:T(8,128)}, f32[3,32,256]{2,1,0:T(8,128)}, f32[32,256]{1,0:T(8,128)}) custom-call(s32[32]{0:T(128)} %get-tuple-element.22.slot_ref, f32[128,7,4,128]{3,2,1,0:T(4,128)} %last_exchange.1.recv_ref), custom_call_target="tpu_custom_call" | custom-call | tf_op jit(solution)/shard_map/unpack/pallas_call | solution.py:760
  (9 shorter events, 0.2 us)

commit v5 on v4

--- a/solution.py
+++ b/solution.py
@@ -289,17 +289,20 @@
 
 def bounds(table_ref, low_ref, high_ref):
     blocks, cells = table_ref.shape[0], table_ref.shape[1]
-
-    def one(cell, carry):
-        for block in range(blocks):
-            rows = table_ref[block, cell]
-            low = jnp.broadcast_to(jnp.min(rows, axis=1, keepdims=True), (8, LANES))
-            high = jnp.broadcast_to(jnp.max(rows, axis=1, keepdims=True), (8, LANES))
+    together = 4
+
+    def some(step, carry):
+        which = [(block, step * together + n) for n in range(together) for block in range(blocks)]
+        lows = [jnp.min(table_ref[block, cell], axis=1, keepdims=True) for block, cell in which]
+        highs = [jnp.max(table_ref[block, cell], axis=1, keepdims=True) for block, cell in which]
+        for (block, cell), low, high in zip(which, lows, highs):
+            low = jnp.broadcast_to(low, (8, LANES))
+            high = jnp.broadcast_to(high, (8, LANES))
             low_ref[block * cells + cell] = jnp.minimum(low, pltpu.roll(low, 4, 0))
             high_ref[block * cells + cell] = jnp.maximum(high, pltpu.roll(high, 4, 0))
         return carry
 
-    lax.fori_loop(0, cells, one, 0)
+    lax.fori_loop(0, cells // together, some, 0)
 
 
 def middle(low, high):
@@ -388,14 +391,14 @@
 
 
 def lane_sums(acc):
-    ones = jnp.ones((8, LANES), jnp.bfloat16)
-    total = jnp.zeros((8, 2 * LANES), jnp.float32)
-    for part in reversed(three_parts(acc)):
-        total = total + lax.dot_general(
-            ones, part.astype(jnp.bfloat16), (((1,), (1,)), ((), ())),
-            preferred_element_type=jnp.float32,
-        )
-    return [total[0:1, 0:LANES], total[0:1, LANES : 2 * LANES]]
+    halves = []
+    for half in range(2):
+        part = acc[half * LANES : (half + 1) * LANES, :].T
+        eight = part[0:8]
+        for row in range(8, LANES, 8):
+            eight = eight + part[row : row + 8]
+        halves.append(jnp.sum(eight, axis=0, keepdims=True))
+    return halves
 
 
 def fast_density(cells, partners, mass, box, near_ref, count_ref, table_ref, low_ref, high_ref, rho_ref,
@@ -403,7 +406,7 @@
     lengths = by_row(box + (1.0,))
     step = 64
 
-    def one_cell(cell, carry):
+    def one_cell(cell, own_ref, factor_ref, acc_ref):
         low_a, high_a = low_ref[cell], high_ref[cell]
         origin = middle(low_a, high_a)
         own_factors(table_ref[0, cell], origin, own_ref)
@@ -423,9 +426,13 @@
         h = halves_of(table_ref.at[0], cell, 3)
         for half, (part, total) in enumerate(zip(h, lane_sums(acc_ref[...]))):
             rho_ref[cell, half : half + 1] = mass * (1.0 + total) / (part * part * part)
+
+    def two_cells(pair, carry):
+        for number in range(2):
+            one_cell(2 * pair + number, own_ref.at[number], factor_ref.at[number], acc_ref.at[number])
         return carry
 
-    lax.fori_loop(0, cells, one_cell, 0)
+    lax.fori_loop(0, cells // 2, two_cells, 0)
 
 
 def fast_accel(cells, partners, mass, box, near_ref, count_ref, slot_ref, table_ref, low_ref, high_ref,
@@ -434,7 +441,7 @@
     lengths = by_row(box + (1.0,))
     step = 32
 
-    def one_cell(cell, carry):
+    def one_cell(cell, own_ref, factor_ref, moved_ref, ai_ref, acc_refs):
         low_a, high_a = low_ref[cell], high_ref[cell]
         origin = middle(low_a, high_a)
         centred = own_factors(table_ref[0, cell], origin, own_ref)
@@ -480,18 +487,24 @@
         for half in range(2):
             row = slice(4 * half + 3, 4 * half + 4)
             q_ref[cell, row] = rho_ref[0, cell, half : half + 1]
+
+    def two_cells(pair, carry):
+        for number in range(2):
+            one_cell(2 * pair + number, own_ref.at[number], factor_ref.at[number], moved_ref.at[number], ai_ref.at[number], [ref.at[number] for ref in acc_refs])
         return carry
 
-    lax.fori_loop(0, cells, one_cell, 0)
-
-
-def density_kernel(partners, mass, unit, shifts, box, near_ref, count_ref, table_ref, rho_ref,
+    lax.fori_loop(0, cells // 2, two_cells, 0)
+
+
+def density_kernel(partners, mass, unit, shifts, box, near_ref, count_ref, table_ref, rho_ref, fits_ref,
                    low_ref, high_ref, own_ref, factor_ref,
                    fixed_ref, list_ref, xi_ref, yi_ref, zi_ref, ci_ref, acc_ref):
     cells = table_ref.shape[1]
     bounds(table_ref, low_ref, high_ref)
     fits = one_image(cells, partners, box, near_ref, low_ref, high_ref)
 
+    fits_ref[0] = jnp.where(fits, 1, 0)
+
     @pl.when(fits)
     def _():
         fast_density(cells, partners, mass, box, near_ref, count_ref, table_ref, low_ref, high_ref,
@@ -500,7 +513,7 @@
     @pl.when(jnp.logical_not(fits))
     def _():
         any_density(partners, mass, unit, shifts, box, near_ref, count_ref, table_ref, rho_ref,
-                    fixed_ref, list_ref, xi_ref, yi_ref, zi_ref, ci_ref, acc_ref)
+                    fixed_ref, list_ref, xi_ref, yi_ref, zi_ref, ci_ref, acc_ref.at[0])
 
 
 def any_density(partners, mass, unit, shifts, box, near_ref, count_ref, table_ref, rho_ref,
@@ -546,14 +559,14 @@
     lax.fori_loop(0, cells, one_cell, 0)
 
 
-def accel_kernel(partners, mass, unit, shifts, box, near_ref, count_ref, slot_ref, table_ref, rho_ref,
+def accel_kernel(partners, mass, unit, shifts, box, near_ref, count_ref, slot_ref, fits_ref, table_ref, rho_ref,
                  recv_ref, q_ref, v_ref,
                  low_ref, high_ref, own_ref, factor_ref, moved_ref, sum_ref,
                  fixed_ref, inverse_ref, list_ref, inverse_list_ref, xi_ref, yi_ref, zi_ref, ci_ref, ai_ref,
                  ax_ref, ay_ref, az_ref):
     cells = table_ref.shape[1]
     bounds(table_ref, low_ref, high_ref)
-    fits = one_image(cells, partners, box, near_ref, low_ref, high_ref)
+    fits = fits_ref[0] > 0
 
     def invert(cell, carry):
         for block in range(rho_ref.shape[0]):
@@ -572,7 +585,7 @@
     def _():
         any_accel(partners, mass, unit, shifts, box, near_ref, count_ref, slot_ref, table_ref, rho_ref,
                   recv_ref, q_ref, v_ref, fixed_ref, inverse_ref, list_ref, inverse_list_ref,
-                  xi_ref, yi_ref, zi_ref, ci_ref, ai_ref, ax_ref, ay_ref, az_ref)
+                  xi_ref, yi_ref, zi_ref, ci_ref, ai_ref.at[0], ax_ref.at[0], ay_ref.at[0], az_ref.at[0])
 
 
 def any_accel(partners, mass, unit, shifts, box, near_ref, count_ref, slot_ref, table_ref, rho_ref,
@@ -705,17 +718,17 @@
     square = (particles, LANES)
     columns = [pltpu.VMEM(square, jnp.int32)] * 3
     extent = [pltpu.VMEM((7 * cell_count, 8, LANES), jnp.float32)] * 2 + [
-        pltpu.VMEM((particles, 32), jnp.bfloat16),
-        pltpu.VMEM((partners, 32, particles), jnp.bfloat16),
+        pltpu.VMEM((2, particles, 32), jnp.bfloat16),
+        pltpu.VMEM((2, partners, 32, particles), jnp.bfloat16),
     ]
     fixed = pltpu.VMEM((7 * cell_count, 8, LANES), jnp.int32)
-    rho = pl.pallas_call(
+    rho, fits = pl.pallas_call(
         functools.partial(density_kernel, partners, mass, unit, shifts, box),
-        out_shape=f32(cell_count, 2, LANES),
+        out_shape=[f32(cell_count, 2, LANES), jax.ShapeDtypeStruct((1,), jnp.int32)],
         in_specs=[smem, smem, vmem],
-        out_specs=vmem,
+        out_specs=[vmem, smem],
         scratch_shapes=extent + [fixed, pltpu.VMEM((chunks, 4, LANES), jnp.int32)] + columns
-        + [pltpu.VMEM(square, jnp.float32)] * 2,
+        + [pltpu.VMEM(square, jnp.float32), pltpu.VMEM((2,) + square, jnp.float32)],
         name="density",
     )(near, table_count, table)
 
@@ -732,21 +745,22 @@
     out_q, out_v = pl.pallas_call(
         functools.partial(accel_kernel, partners, mass, unit, shifts, box),
         out_shape=[f32(cell_count, 8, LANES)] * 2,
-        in_specs=[smem, smem, smem, vmem, vmem, vmem],
+        in_specs=[smem, smem, smem, smem, vmem, vmem, vmem],
         out_specs=[vmem, vmem],
         scratch_shapes=extent
         + [
-            pltpu.VMEM((partners, 8, LANES), jnp.float32),
-            pltpu.VMEM(square, jnp.float32),
+            pltpu.VMEM((2, partners, 8, LANES), jnp.float32),
+            pltpu.VMEM((2,) + square, jnp.float32),
             fixed,
             pltpu.VMEM((7 * cell_count, 2, LANES), jnp.float32),
             pltpu.VMEM((chunks, 4, LANES), jnp.int32),
             pltpu.VMEM((chunks, 1, LANES), jnp.float32),
         ]
         + columns
-        + [pltpu.VMEM(square, jnp.float32)] * 5,
+        + [pltpu.VMEM(square, jnp.float32)]
+        + [pltpu.VMEM((2,) + square, jnp.float32)] * 4,
         name="accel",
-    )(near, table_count, slot_before, table, table_rho, recv)
+    )(near, table_count, slot_before, fits, table, table_rho, recv)
 
     last = pl.pallas_call(
         functools.partial(last_exchange_kernel, sizes),

time: 181 us -> 159 us (0.88)
  Pallas kernels: 169 us -> 147 us
    pallas_call x1, Pallas kernels: 54.7 us -> 42.8 us  [shards(): pl.pallas_call(functools.partial(accel_kernel, partners, mass, unit, shif...]
    pallas_call x1, Pallas kernels: 29.6 us -> 19.7 us  [shards(): pl.pallas_call(functools.partial(density_kernel, partners, mass, unit, sh...]
where the time goes in v5:
time: 159 us; the launch traced here: 158 us
  Pallas kernels  147 us (92%)
  other arithmetic  7.15 us (4%)
  local copies, waits for them, and re-layouts  3.57 us (2%)
    pallas_call x1, Pallas kernels, shards(): pl.pallas_call(functools.partial(accel_kernel, partners, mass, unit, shif...  42.8 us
    pallas_call x1, Pallas kernels, shards(): pl.pallas_call(functools.partial(first_exchange_kernel, sizes), out_shape...  35.7 us
    pallas_call x1, Pallas kernels, shards(): pl.pallas_call(functools.partial(last_exchange_kernel, sizes), out_shape=...  30.1 us
    pallas_call x1, Pallas kernels, shards(): pl.pallas_call(functools.partial(density_kernel, partners, mass, unit, sh...  19.7 us
    pallas_call x1, Pallas kernels, shards(): pl.pallas_call(functools.partial(cell_halo_kernel, sizes), out_shape=[f32...  9.22 us
    pallas_call x1, Pallas kernels, shards(): pl.pallas_call(functools.partial(rho_halo_kernel, sizes), out_shape=f32(7...  6.94 us

profile of v5, /device:TPU:1, one launch (start us, length us, event | category | flops | bytes accessed | tf_op | source)
XLA Modules:
  0.0 158.4 jit_solution(18399196195357255144)
XLA Ops:
  0.8 0.7 and_select_fusion.2
  1.5 0.7 fusion.1
  2.2 0.2 convert_reduce_fusion
  2.4 0.7 multiply_add_fusion
  3.1 0.1 add.151
  3.2 1.3 add_bitcast_fusion.meta_ref
  4.5 0.1 select_reduce_fusion.2
  4.6 0.6 fusion.3
  5.1 0.1 copy.20
  5.2 0.7 reshape.214.near_ref
  5.9 35.7 %first_exchange.1 = (f32[128,7,4,128]{3,2,1,0:T(4,128)}, s32[128,1,128]{2,1,0:T(1,128)}) custom-call(s32[256]{0:T(256)} %bitcast.17, s32[1,128]{1,0:T(1,128)} %add_bitcast_fusion.meta_ref, f32[3,32,256]{2,1,0:T(8,128)} %bitcast.14, f32[32,256]{1,0:T(8,128)} %h_ref.1, f32[3,32,256]{2,1,0:T(8,128)} %bitcast.15), custom_call_target="tpu_custom_call" | custom-call | tf_op jit(solution)/shard_map/first_exchange/pallas_call | solution.py:680
  41.6 1.1 and_add_fusion
  42.9 0.1 copy.17
  43.0 1.8 %select_reduce_fusion = (s32[32]{0:T(128)S(1)}, s32[32]{0:T(128)}) fusion(s32[128,32]{0,1:T(8,128)S(1)} %copy.24, s32[128,32]{0,1:T(8,128)S(1)} %copy.22, s32[32]{0:T(128)S(1)} %iota_add_fusion, s32[128,32]{0,1:T(8,128)S(1)} %copy.19, s32[128,32]{0,1:T(8,128)S(1)} %copy.17), kind=kLoop, calls=%fused_computation | loop fusion | flops 786368 | bytes 65920 | tf_op jit(solution)/shard_map/reduce_sum | solution.py:699
  44.8 0.5 and_select_fusion
  45.4 0.5 pad_bitcast_fusion.count_ref
  45.9 9.2 %cell_halo.1 = (f32[7,32,8,128]{3,2,1,0:T(8,128)}, s32[7,1,128]{2,1,0:T(1,128)}) custom-call(s32[32]{0:T(128)} %get-tuple-element.36.slot_ref, s32[1,128]{1,0:T(1,128)} %pad_bitcast_fusion.count_ref, f32[128,7,4,128]{3,2,1,0:T(4,128)} %get-tuple-element.15.recv_ref), custom_call_target="tpu_custom_call" | custom-call | tf_op jit(solution)/shard_map/cell_halo/pallas_call | solution.py:706
  55.1 0.7 slice_reduce_fusion
  55.8 0.7 reshape_squeeze.3.count_ref
  56.5 19.7 %density.1 = (f32[32,2,128]{2,1,0:T(2,128)}, s32[1]{0:T(128)}) custom-call(s32[288]{0:T(512)} %reshape.214.near_ref, s32[224]{0:T(256)} %reshape_squeeze.3.count_ref, f32[7,32,8,128]{3,2,1,0:T(8,128)} %get-tuple-element.17.table_ref), custom_call_target="tpu_custom_call" | custom-call | tf_op jit(solution)/shard_map/density/pallas_call | solution.py:725
  76.2 6.9 %rho_halo.1.rho_ref = f32[7,32,2,128]{3,2,1,0:T(2,128)} custom-call(f32[32,2,128]{2,1,0:T(2,128)} %get-tuple-element.19.rho_ref), custom_call_target="tpu_custom_call" | custom-call | tf_op jit(solution)/shard_map/rho_halo/pallas_call | solution.py:735
  83.1 42.8 %accel.1 = (f32[32,8,128]{2,1,0:T(8,128)}, f32[32,8,128]{2,1,0:T(8,128)}) custom-call(s32[288]{0:T(512)} %reshape.214.near_ref, s32[224]{0:T(256)} %reshape_squeeze.3.count_ref, s32[32]{0:T(128)} %get-tuple-element.36.slot_ref, s32[1]{0:T(128)} %get-tuple-element.18.fits_ref, f32[7,32,8,128]{3,2,1,0:T(8,128)} %get-tuple-element.17.table_ref, ...), custom_call_target="tpu_custom_call" | custom-call | tf_op jit(solution)/shard_map/accel/pallas_call | solution.py:745
  125.9 30.1 %last_exchange.1.recv_ref = f32[128,7,4,128]{3,2,1,0:T(4,128)} custom-call(s32[256]{0:T(256)} %bitcast.16, f32[32,8,128]{2,1,0:T(8,128)} %get-tuple-element.20.q_ref, f32[32,8,128]{2,1,0:T(8,128)} %get-tuple-element.21.v_ref), custom_call_target="tpu_custom_call" | custom-call | tf_op jit(solution)/shard_map/last_exchange/pallas_call | solution.py:765
  156.0 2.4 %unpack.1 = (f32[3,32,256]{2,1,0:T(8,128)}, f32[3,32,256]{2,1,0:T(8,128)}, f32[32,256]{1,0:T(8,128)}) custom-call(s32[32]{0:T(128)} %get-tuple-element.26.slot_ref, f32[128,7,4,128]{3,2,1,0:T(4,128)} %last_exchange.1.recv_ref), custom_call_target="tpu_custom_call" | custom-call | tf_op jit(solution)/shard_map/unpack/pallas_call | solution.py:774
  (9 shorter events, 0.2 us)
